TPU v7x, 32 devices: a whole 2x2x4 slice. The times are simulated.
32 devices in a mesh: dp: 4 (over y, core), expert: 8 (over z, x).
Axes of the slice: x: 2, y: 2, z: 4, core: 2. Of those that a mesh axis runs over, the one named last changes fastest.
Arguments:
- hidden: bfloat16 [8192, 768], P(('dp', 'expert')), may hold values from -6 to 6
- w_down: bfloat16 [8, 768, 2048], P('expert', 'dp'), may hold values from -0.21875 to 0.21875
- expert_ids: int32 [1024, 4], P(('dp', 'expert')), may hold values from 0 to 7, all different within a row; in each aligned block of 32 rows (0 to 31, 32 to 63, ...) at most 32 rows name the same one
- gates: float32 [1024, 4], P(('dp', 'expert')), may hold values from 0.05 to 1
- cotangent: bfloat16 [1024, 2048], P(('dp', 'expert')), may hold values from -6 to 6
Outputs:
- mixed: bfloat16 [1024, 2048], P(('dp', 'expert'))
- gate_grads: float32 [1024, 4], P(('dp', 'expert'))
- hidden_grads: bfloat16 [8192, 768], P(('dp', 'expert'))
- weight_grads: bfloat16 [8, 768, 2048], P('expert', 'dp')
Inputs may be any that keep to these rules, and one draw needn't show every extreme that they name: `expert_ids`: each row names 4 different experts. Among the rows of one device no expert is named more than 32 times, a bound that some block reaches.
All inputs are finite; a program needn't handle non-finite values.
Results may differ from a plain program's by a relative error of at most 0.015.
Values may be sent and summed in bfloat16 or wider, within the bound.
A program may use at most 64 MiB of HBM per device.

v0:
```python
import functools

import jax
import jax.numpy as jnp
from jax import lax
from jax.experimental import pallas as pl
from jax.experimental.pallas import tpu as pltpu
from jax.sharding import PartitionSpec as P

MESH = pl.DeviceIdType.MESH
F32 = jnp.float32
BF16 = jnp.bfloat16


VMEM_BYTES = 67043328


def kernel(
    nd, ne, C,
    hidden_in, w, ids, gates, cot,
    mixed, gate_grads, hidden_grads, weight_grads,
    hidden, wfull, cot_all, meta_send, meta_recv, gg_send, gg_recv,
    ht, gh, ght, z, wg_send1, wg_recv1, wg_send2, wg_recv2, wg_own,
    mx_send1, mx_recv1, mx_send2, mx_recv2, mx_own,
    wy_s, wy_r, wf_s, wf_r, cz_s, cz_r, cf_s, cf_r, me_s, me_r, gg_s, gg_r,
    g1_s, g1_r, g2_s, g2_r, m1_s, m1_r, m2_s, m2_r, lw, lc, lh,
):
    R, N = nd // 2, ne // 2
    rows, D = w.shape
    topk, tok = ids.shape
    F = hidden.shape[1]
    cap = hidden.shape[0] // ne
    T, cw = ne * tok, D // C
    a, e = lax.axis_index("dp"), lax.axis_index("expert")
    r, c = a // 2, a % 2
    q, x = e // 2, e % 2

    def to(a2, e2):
        return {"dp": a2, "expert": e2}

    def remote(src, dst, ss, rs, dev):
        copy = pltpu.make_async_remote_copy(
            src_ref=src, dst_ref=dst, send_sem=ss, recv_sem=rs, device_id=dev, device_id_type=MESH
        )
        copy.start()
        return copy

    def w_rows(block):
        return pl.ds(pl.multiple_of(block * rows, rows), rows)

    def cols(j):
        return slice(j * cw, (j + 1) * cw)

    barrier = pltpu.get_barrier_semaphore()
    for d in range(1, ne):
        pl.semaphore_signal(barrier, inc=1, device_id=to(a, (e + d) % ne), device_id_type=MESH)
    for d in range(1, R):
        pl.semaphore_signal(barrier, inc=1, device_id=to(((r + d) % R) * 2 + c, e), device_id_type=MESH)
    pl.semaphore_signal(barrier, inc=1, device_id=to(r * 2 + 1 - c, e), device_id_type=MESH)
    own_w, own_c = [], []
    for j in range(C):
        own_w.append(pltpu.make_async_copy(w.at[:, cols(j)], wfull.at[j, w_rows(a)], lw.at[j]))
        own_c.append(pltpu.make_async_copy(cot.at[:, cols(j)], cot_all.at[j, q, x], lc.at[j]))
        own_w[j].start()
        own_c[j].start()
    own_h = pltpu.make_async_copy(hidden_in, hidden, lh.at[0])
    own_h.start()

    eye = lax.broadcasted_iota(jnp.int32, (tok, tok), 0) == lax.broadcasted_iota(jnp.int32, (tok, tok), 1)
    upper = (
        lax.broadcasted_iota(jnp.int32, (tok, tok), 0) < lax.broadcasted_iota(jnp.int32, (tok, tok), 1)
    ).astype(F32)

    def to_row(col):
        return jnp.sum(jnp.where(eye, col, 0.0), axis=0, keepdims=True)

    def to_col(row):
        return jnp.sum(jnp.where(eye, row, 0.0), axis=1, keepdims=True)

    idf = ids[...].astype(F32)
    gat = gates[...]
    names = lax.broadcasted_iota(jnp.int32, (ne, tok), 0).astype(F32)
    id_rows = [idf[k : k + 1, :] for k in range(topk)]
    choose = jnp.zeros((ne, tok), F32)
    gate_t = jnp.zeros((ne, tok), F32)
    for k in range(topk):
        hit = id_rows[k] == names
        choose = choose + jnp.where(hit, 1.0, 0.0)
        gate_t = gate_t + jnp.where(hit, gat[k : k + 1, :], 0.0)
    position = jnp.dot(choose.astype(BF16), upper.astype(BF16), preferred_element_type=F32)
    slot_t = jnp.where(choose > 0.0, position, -1.0)
    meta_send[...] = jnp.zeros_like(meta_send)
    gg_send[...] = jnp.zeros_like(gg_send)
    for k in range(ne):
        meta_send[k // 2, k % 2, 0:1, 0:tok] = slot_t[k : k + 1, :]
        meta_send[k // 2, k % 2, 1:2, 0:tok] = gate_t[k : k + 1, :]
    meta_recv[q, x] = meta_send[q, x]

    pl.semaphore_wait(barrier, ne - 1 + R - 1 + 1)

    wy, wf, cz, cf, me, g1, g2, m1, m2, gg = ({} for _ in range(10))
    order = sorted(range(1, N), key=lambda d: min(d, N - d))
    pair_e, pair_d = to(a, q * 2 + 1 - x), to(r * 2 + 1 - c, e)
    for d in range(1, ne):
        o = (e + d) % ne
        me[d] = remote(
            meta_send.at[o // 2, o % 2], meta_recv.at[q, x], me_s.at[d - 1], me_r.at[d - 1], to(a, o)
        )
    for j in range(C):
        own_w[j].wait()
        own_c[j].wait()
        mine = wfull.at[j, w_rows(a)]
        for d in range(1, R):
            wy[d, j] = remote(
                mine, mine, wy_s.at[d - 1, j], wy_r.at[d - 1, j], to(((r + d) % R) * 2 + c, e)
            )
        ours = cot_all.at[j, q, x]
        for d in order:
            cz[d, j] = remote(
                ours, ours, cz_s.at[d - 1, j], cz_r.at[d - 1, j], to(a, ((q + d) % N) * 2 + x)
            )
        cf[0, j] = remote(ours, ours, cf_s.at[0, j], cf_r.at[0, j], pair_e)
        wf[0, j] = remote(mine, mine, wf_s.at[0, j], wf_r.at[0, j], pair_d)

    def forward_cot(j):
        for d in order:
            block = cot_all.at[j, (q - d + N) % N, x]
            cz[d, j].wait_recv()
            cf[d, j] = remote(block, block, cf_s.at[d, j], cf_r.at[d, j], pair_e)

    def forward_w(j):
        for d in range(1, R):
            block = wfull.at[j, w_rows(((r - d + R) % R) * 2 + c)]
            wy[d, j].wait_recv()
            wf[d, j] = remote(block, block, wf_s.at[d, j], wf_r.at[d, j], pair_d)

    own_h.wait()
    for d in range(1, ne):
        me[d].wait_recv()

    def route(b):
        return meta_recv[b // 2, b % 2, 0:1, 0:tok], meta_recv[b // 2, b % 2, 1:2, 0:tok]

    def placer(slot_row):
        return (lax.broadcasted_iota(jnp.int32, (cap, tok), 0).astype(F32) == slot_row).astype(BF16)

    for b in range(ne):
        slot_row, gate_row = route(b)
        rows_b = lax.dot_general(
            placer(slot_row), hidden[b * cap : (b + 1) * cap, :], (((0,), (0,)), ((), ())),
            preferred_element_type=F32,
        )
        ht[b // 2, b % 2] = rows_b.astype(BF16)
        gh[b // 2, b % 2] = (to_col(gate_row) * rows_b).astype(BF16)
    ght[...] = gh[...].reshape(T, F).astype(F32).T.astype(BF16)

    def cot_part(j):
        forward_cot(j)

    def grads_part(j):
        for d in range(N):
            cf[d, j].wait_recv()
        right = cot_all[j].reshape(T, cw)

        def block_of(block):
            return jnp.dot(ght[w_rows(block), :], right, preferred_element_type=F32)

        for k in range(R):
            wg_send1[j, k] = block_of(((r + k) % R) * 2 + 1 - c).astype(BF16)
        g1[j] = remote(wg_send1.at[j], wg_recv1.at[j], g1_s.at[j], g1_r.at[j], pair_d)
        for k in range(R):
            val = block_of(((r + k) % R) * 2 + c)
            if k == 0:
                wg_own[j] = val
            else:
                wg_hold = val
                if k == 1:
                    g1[j].wait_recv()
                wg_send2[j, k - 1] = (wg_hold + wg_recv1[j, k].astype(F32)).astype(BF16)
                g2[k, j] = remote(
                    wg_send2.at[j, k - 1], wg_recv2.at[j, k - 1], g2_s.at[k - 1, j], g2_r.at[k - 1, j],
                    to(((r + k) % R) * 2 + c, e),
                )
        if R == 1:
            g1[j].wait_recv()

    def out_part(j):
        forward_w(j)
        for d in range(R):
            wf[d, j].wait_recv()
        left = gh[:, pl.ds(1 - x, 1)].reshape(N * tok, F)
        val = jnp.dot(left, wfull[j], preferred_element_type=F32)
        mx_send1[j] = val.astype(BF16).reshape(N, tok, cw)
        m1[j] = remote(mx_send1.at[j], mx_recv1.at[j], m1_s.at[j], m1_r.at[j], pair_e)
        left = gh[:, pl.ds(x, 1)].reshape(N * tok, F)
        val = jnp.dot(left, wfull[j], preferred_element_type=F32)
        mx_own[j] = val.reshape(N, tok, cw)

    def z_part(j):
        val = lax.dot_general(
            cot_all[j].reshape(T, cw), wfull[j], (((1,), (1,)), ((), ())), preferred_element_type=F32
        )
        z[...] = val if j == 0 else z[...] + val

    def mix_part(j):
        m1[j].wait_recv()
        for k in order:
            o = (q + k) % N
            mx_send2[j, o] = (mx_own[j, o] + mx_recv1[j, o].astype(F32)).astype(BF16)
            m2[k, j] = remote(
                mx_send2.at[j, o], mx_recv2.at[j, q], m2_s.at[k - 1, j], m2_r.at[k - 1, j],
                to(a, o * 2 + x),
            )

    cot_part(0)
    for j in range(C):
        if j + 1 < C:
            cot_part(j + 1)
        out_part(j)
        grads_part(j)
        z_part(j)
        if j > 0:
            mix_part(j - 1)
    mix_part(C - 1)

    for b in range(ne):
        zb = z[b * tok : (b + 1) * tok, :]
        slot_row, gate_row = route(b)
        gg_col = jnp.sum(ht[b // 2, b % 2].astype(F32) * zb, axis=1, keepdims=True)
        gg_send[b // 2, b % 2, 0:1, 0:tok] = to_row(gg_col)
        scaled = (to_col(gate_row) * zb).astype(BF16)
        hidden_grads[b * cap : (b + 1) * cap, :] = jnp.dot(
            placer(slot_row), scaled, preferred_element_type=F32
        ).astype(BF16)
    for d in range(1, ne):
        o = (e + d) % ne
        gg[d] = remote(
            gg_send.at[o // 2, o % 2], gg_recv.at[q, x], gg_s.at[d - 1], gg_r.at[d - 1], to(a, o)
        )
    gg_recv[q, x] = gg_send[q, x]

    for j in range(C):
        total = mx_own[j, q] + mx_recv1[j, q].astype(F32)
        for k in order:
            m2[k, j].wait_recv()
            total = total + mx_recv2[j, (q - k + N) % N].astype(F32)
        mixed[:, cols(j)] = total.astype(BF16)

    for d in range(1, ne):
        gg[d].wait_recv()
    for k in range(topk):
        row = jnp.zeros((1, tok), F32)
        for b in range(ne):
            row = row + jnp.where(id_rows[k] == float(b), gg_recv[b // 2, b % 2, 0:1, 0:tok], 0.0)
        gate_grads[k : k + 1, :] = row

    for j in range(C):
        val = wg_own[j] + wg_recv1[j, 0].astype(F32)
        for k in range(1, R):
            g2[k, j].wait_recv()
            val = val + wg_recv2[j, k - 1].astype(F32)
        weight_grads[:, cols(j)] = val.astype(BF16)

    for group in (wy, wf, cz, cf, me, g1, g2, m1, m2, gg):
        for copy in group.values():
            copy.wait_send()


def store_kernel(count, *refs):
    sems = refs[-1]
    copies = [pltpu.make_async_copy(refs[i], refs[count + i], sems.at[i]) for i in range(count)]
    for copy in copies:
        copy.start()
    for copy in copies:
        copy.wait()


def fused(hidden, weight_rows, expert_ids, gates, cotangent):
    nd, ne = lax.axis_size("dp"), lax.axis_size("expert")
    rows, D = weight_rows.shape
    tok, topk = expert_ids.shape
    F = hidden.shape[1]
    T, R, N = ne * tok, nd // 2, ne // 2
    C = 4
    while D % (C * 128):
        C //= 2
    cw = D // C
    vm = pltpu.VMEM
    sem = lambda *n: pltpu.SemaphoreType.DMA(tuple(max(i, 1) for i in n))
    near, far = pl.BlockSpec(memory_space=pltpu.VMEM), pl.BlockSpec(memory_space=pltpu.HBM)
    shapes = [((tok, D), BF16), ((topk, tok), F32), (hidden.shape, BF16), ((rows, D), BF16)]
    last = max(R - 1, 1)
    result_bytes = 2 * (tok * D + hidden.size + rows * D) + 128 * 1024
    results = pl.pallas_call(
        functools.partial(kernel, nd, ne, C),
        out_shape=tuple(pltpu.VMEM(*s) for s in shapes),
        in_specs=[far, far, near, near, far],
        out_specs=(near,) * 4,
        scratch_shapes=[
            vm(hidden.shape, BF16), vm((C, F, cw), BF16), vm((C, N, 2, tok, cw), BF16),
            vm((N, 2, 8, 128), F32), vm((N, 2, 8, 128), F32),
            vm((N, 2, 8, 128), F32), vm((N, 2, 8, 128), F32),
            vm((N, 2, tok, F), BF16), vm((N, 2, tok, F), BF16), vm((F, T), BF16), vm((T, F), F32),
            vm((C, R, rows, cw), BF16), vm((C, R, rows, cw), BF16),
            vm((C, last, rows, cw), BF16), vm((C, last, rows, cw), BF16), vm((C, rows, cw), F32),
            vm((C, N, tok, cw), BF16), vm((C, N, tok, cw), BF16),
            vm((C, N, tok, cw), BF16), vm((C, N, tok, cw), BF16), vm((C, N, tok, cw), F32),
            sem(R - 1, C), sem(R - 1, C), sem(R, C), sem(R, C),
            sem(N - 1, C), sem(N - 1, C), sem(N, C), sem(N, C),
            sem(ne - 1), sem(ne - 1), sem(ne - 1), sem(ne - 1),
            sem(C), sem(C), sem(R - 1, C), sem(R - 1, C),
            sem(C), sem(C), sem(N - 1, C), sem(N - 1, C), sem(C), sem(C), sem(1),
        ],
        compiler_params=pltpu.CompilerParams(
            collective_id=0, has_side_effects=True, vmem_limit_bytes=VMEM_BYTES - result_bytes
        ),
    )(hidden, weight_rows, expert_ids.T, gates.T, cotangent)
    mixed, gate_grads, hidden_grads, sums = pl.pallas_call(
        functools.partial(store_kernel, len(shapes)),
        out_shape=tuple(jax.ShapeDtypeStruct(*s) for s in shapes),
        in_specs=[pl.BlockSpec(memory_space=pl.ANY)] * 4,
        out_specs=(far,) * 4,
        scratch_shapes=[sem(len(shapes))],
        compiler_params=pltpu.CompilerParams(vmem_limit_bytes=1024 * 1024),
    )(*results)
    return mixed, gate_grads.T, hidden_grads, sums


def slot_table(expert_ids, experts, capacity):
    flat_ids = expert_ids.reshape(-1)
    choose = (flat_ids[:, None] == jnp.arange(experts, dtype=jnp.int32)[None, :]).astype(jnp.int32)
    earlier = jnp.cumsum(choose, axis=0) - choose
    position = jnp.sum(earlier * choose, axis=1)
    target = flat_ids * capacity + position
    return (target[None, :] == jnp.arange(experts * capacity, dtype=jnp.int32)[:, None]).astype(BF16)


def plain(hidden, weight_rows, expert_ids, gates, cotangent):
    experts = lax.axis_size("expert")
    capacity = hidden.shape[0] // experts
    tok, topk = expert_ids.shape
    width = cotangent.shape[1]
    table = slot_table(expert_ids, experts, capacity)
    weight = lax.all_gather(weight_rows, "dp", axis=0, tiled=True)
    outputs = jnp.dot(hidden, weight, preferred_element_type=F32).astype(BF16)
    back = lax.all_to_all(outputs, "expert", split_axis=0, concat_axis=0, tiled=True)
    picked = lax.dot_general(table, back, (((0,), (0,)), ((), ())), preferred_element_type=F32)
    picked = picked.reshape(tok, topk, width)
    cot32 = cotangent.astype(F32)[:, None, :]
    mixed = jnp.sum(gates[:, :, None] * picked, axis=1).astype(BF16)
    gate_grads = jnp.sum(picked * cot32, axis=2)
    routed = (gates[:, :, None] * cot32).astype(BF16).reshape(-1, width)
    packed = jnp.dot(table, routed, preferred_element_type=F32).astype(BF16)
    grads = lax.all_to_all(packed, "expert", split_axis=0, concat_axis=0, tiled=True)
    hidden_grads = lax.dot_general(
        grads, weight, (((1,), (1,)), ((), ())), preferred_element_type=F32
    ).astype(BF16)
    partial = lax.dot_general(
        hidden, grads, (((0,), (0,)), ((), ())), preferred_element_type=F32
    ).astype(BF16)
    sums = lax.psum_scatter(partial, "dp", scatter_dimension=0, tiled=True)
    return mixed, gate_grads, hidden_grads, sums


def per_device(hidden, w_down, expert_ids, gates, cotangent):
    nd, ne = lax.axis_size("dp"), lax.axis_size("expert")
    rows, width = w_down.shape[1:]
    cap, tok = hidden.shape[0] // ne, expert_ids.shape[0]
    tiled = rows % 16 == 0 and cap % 16 == 0 and tok % 16 == 0 and tok <= 128
    paired = nd % 2 == 0 and ne % 2 == 0
    body = fused if tiled and paired else plain
    mixed, gate_grads, hidden_grads, sums = body(
        hidden, w_down.reshape(rows, width), expert_ids, gates, cotangent
    )
    return mixed, gate_grads, hidden_grads, sums.reshape(1, rows, width)


def solution(mesh):
    split = P(("dp", "expert"), None)
    weights = P("expert", "dp", None)
    return jax.shard_map(
        per_device,
        mesh=mesh,
        in_specs=(split, weights, split, split, split),
        out_specs=(split, split, split, weights),
        check_vma=False,
    )
```

profile of v0, /device:TPU:0, one launch (start us, length us, event | category | flops | bytes accessed | tf_op | source)
XLA Modules:
  0.0 46.0 jit_solution(8639212226722482709)
XLA Ops:
  0.6 44.3 %shard_map.84 = (bf16[32,2048]{1,0:T(8,128)(2,1)S(1)}, f32[4,32]{1,0:T(4,128)S(1)}, bf16[256,768]{1,0:T(8,128)(2,1)S(1)}, bf16[192,2048]{1,0:T(8,128)(2,1)S(1)}) custom-call(bf16[256,768]{1,0:T(8,128)(2,1)} %hidden_in.1, bf16[192,2048]{1,0:T(8,128)(2,1)} %bitcast.5, s32[4,32]{1,0:T(4,128)} %bitcast.6, f32[4,32]{1,0:T(4,128)} %bitcast.7, bf16[32,2048]{1,0:T(8,128)(2,1)} %cot.1), custom_call_target="tpu_custom_call" | custom-call | tf_op jit(solution)/shard_map/pallas_call | solution.py:294
  45.0 1.1 %shard_map.85 = (bf16[32,2048]{1,0:T(8,128)(2,1)}, f32[4,32]{1,0:T(4,128)}, bf16[256,768]{1,0:T(8,128)(2,1)}, bf16[192,2048]{1,0:T(8,128)(2,1)}) custom-call(bf16[32,2048]{1,0:T(8,128)(2,1)S(1)} %get-tuple-element.12.refs_0_, f32[4,32]{1,0:T(4,128)S(1)} %get-tuple-element.13.refs_1_, bf16[256,768]{1,0:T(8,128)(2,1)S(1)} %get-tuple-element.14.refs_2_, ...), custom_call_target="tpu_custom_call" | custom-call | tf_op jit(solution)/shard_map/pallas_call | solution.py:318
where the time goes:
time: 46.2 us; the launch traced here: 46 us
  Pallas kernels  45.4 us (98%)
  between operations  0.64 us (1%)
    pallas_call x1, Pallas kernels, fused(): pl.pallas_call(functools.partial(kernel, nd, ne, C), out_shape=tuple((plt...  44.3 us
    pallas_call x1, Pallas kernels, fused(): pl.pallas_call(functools.partial(store_kernel, len(shapes)), out_shape=tu...  1.09 us

commit v1 on v0

v1 whole, which is shorter than its diff:
```python
import functools

import jax
import jax.numpy as jnp
from jax import lax
from jax.experimental import pallas as pl
from jax.experimental.pallas import tpu as pltpu
from jax.sharding import PartitionSpec as P

MESH = pl.DeviceIdType.MESH
F32 = jnp.float32
BF16 = jnp.bfloat16


VMEM_BYTES = 67043328


def kernel(
    nd, ne, C, S,
    hidden_in, w, ids, gates, cot,
    mixed, gate_grads, hidden_grads, weight_grads,
    hidden, wfull, cot_all, cot_far, meta, gg_send, gg_recv,
    ht, gh, ght, ght_far, z, wg_send1, wg_recv1, wg_send2, wg_recv2, wg_own, wg_hold,
    mx_send1, mx_recv1, mx_send2, mx_recv2, mx_own,
    wy_s, wy_r, wf_s, wf_r, zs, zr, xs, xr, cy_s, cy_r, hy_s, hy_r, gg_s, gg_r,
    g1_s, g1_r, g2_s, g2_r, m1_s, m1_r, m2_s, m2_r, lw, lc, lh,
):
    N = ne // 2
    rows, D = w.shape
    topk, tok = ids.shape
    F = hidden.shape[1]
    cap = hidden.shape[0] // ne
    T, cw = ne * tok, D // C
    summed = C - S
    a, e = lax.axis_index("dp"), lax.axis_index("expert")
    r, c = a // 2, a % 2
    q, x = e // 2, e % 2

    def to(a2, e2):
        return {"dp": a2, "expert": e2}

    pair_e, pair_c, pair_y = to(a, q * 2 + 1 - x), to(r * 2 + 1 - c, e), to((1 - r) * 2 + c, e)
    ahead, behind = to(a, ((q + 1) % N) * 2 + x), to(a, ((q + N - 1) % N) * 2 + x)
    not_last, not_first = q + 1 < N, q > 0
    onward = ((not_last, ahead), (not_first, behind))

    def copy_of(src, dst, ss, rs, dev):
        return pltpu.make_async_remote_copy(
            src_ref=src, dst_ref=dst, send_sem=ss, recv_sem=rs, device_id=dev, device_id_type=MESH
        )

    def remote(src, dst, ss, rs, dev):
        copy = copy_of(src, dst, ss, rs, dev)
        copy.start()
        return copy

    def w_rows(block):
        return pl.ds(pl.multiple_of(block * rows, rows), rows)

    def cols(j):
        return slice(j * cw, (j + 1) * cw)

    barrier = pltpu.get_barrier_semaphore()
    for dev in (pair_y, pair_c, pair_e):
        pl.semaphore_signal(barrier, inc=1, device_id=dev, device_id_type=MESH)
    for exists, dev in onward:

        @pl.when(exists)
        def _():
            pl.semaphore_signal(barrier, inc=1, device_id=dev, device_id_type=MESH)

    own_w, own_c = [], []
    for j in range(C):
        own_w.append(pltpu.make_async_copy(w.at[:, cols(j)], wfull.at[j, w_rows(a)], lw.at[j]))
        own_c.append(pltpu.make_async_copy(cot.at[:, cols(j)], cot_all.at[j, q, x], lc.at[j]))
        own_w[j].start()
        own_c[j].start()
    own_h = pltpu.make_async_copy(hidden_in, hidden, lh.at[0])
    own_h.start()

    meta[q, x] = jnp.zeros(meta.shape[2:], F32)
    idf = ids[...].astype(F32)
    meta[q, x, 0:topk, 0:tok] = idf
    meta[q, x, topk : 2 * topk, 0:tok] = gates[...]
    gg_send[...] = jnp.zeros_like(gg_send)

    for j in range(C):
        own_w[j].wait()
        own_c[j].wait()

    pl.semaphore_wait(barrier, 3 + not_last.astype(jnp.int32) + not_first.astype(jnp.int32))

    def block(i, zq, xq):
        if i == 0:
            return meta.at[zq, xq]
        if i <= C:
            return cot_all.at[i - 1, zq, xq]
        return cot_far.at[i - 1 - C, zq, xq]

    def line(i, side, d):
        ref = block(i, q + d if side else q - d, x)
        return copy_of(ref, ref, zs.at[i, side, d], zr.at[i, side, d], onward[side][1])

    def arrival(i, side, d):
        ref = block(i, q + d if side else q - d, x)
        return copy_of(ref, ref, zs.at[i, side, d - 1], zr.at[i, side, d - 1], onward[side][1])

    def across(i, zq, xq):
        ref = block(i, zq, xq)
        return copy_of(ref, ref, xs.at[i, zq], xr.at[i, zq], pair_e)

    def there(side, d):
        return q + d < N if side else q >= d

    def begin(i):
        for side in range(2):

            @pl.when(onward[side][0])
            def _():
                line(i, side, 0).start()

        across(i, q, x).start()

    def step(i, d):
        for side in range(2):

            @pl.when(there(side, d))
            def _():
                arrival(i, side, d).wait_recv()
                if d < N - 1:

                    @pl.when(onward[side][0])
                    def _():
                        line(i, side, d).start()

                across(i, q + d if side else q - d, x).start()

    complete = set()

    def gathered(i):
        if i not in complete:
            complete.add(i)
            for zq in range(N):
                across(i, zq, 1 - x).wait_recv()

    def sent(i):
        for side in range(2):
            for d in range(N - 1):

                @pl.when(onward[side][0] & there(side, d))
                def _():
                    line(i, side, d).wait_send()

        for zq in range(N):
            across(i, zq, x).wait_send()

    wy, wf, cy, g1, g2, m1, m2, gg, hy = ({} for _ in range(9))
    order = sorted(range(1, N), key=lambda d: min(d, N - d))

    begin(0)

    def send_w(j):
        mine = wfull.at[j, w_rows(a)]
        wy[j] = remote(mine, mine, wy_s.at[j], wy_r.at[j], pair_y)

    def send_far(s):
        cy[s] = remote(
            cot_all.at[summed + s, q, x], cot_far.at[s, q, x], cy_s.at[s], cy_r.at[s], pair_y
        )

    for j in range(C):
        send_w(j)
        if j == C // 2 - 1:
            for s in range(S):
                send_far(s)
        begin(1 + j)
    for j in range(C):
        mine = wfull.at[j, w_rows(a)]
        wf[0, j] = remote(mine, mine, wf_s.at[0, j], wf_r.at[0, j], pair_c)

    def forward_w(j):
        theirs = wfull.at[j, w_rows((1 - r) * 2 + c)]
        wy[j].wait_recv()
        wf[1, j] = remote(theirs, theirs, wf_s.at[1, j], wf_r.at[1, j], pair_c)

    def placer(slot_row):
        return (lax.broadcasted_iota(jnp.int32, (cap, tok), 0).astype(F32) == slot_row).astype(BF16)

    eye = lax.broadcasted_iota(jnp.int32, (tok, tok), 0) == lax.broadcasted_iota(jnp.int32, (tok, tok), 1)

    def to_row(col):
        return jnp.sum(jnp.where(eye, col, 0.0), axis=0, keepdims=True)

    def to_col(row):
        return jnp.sum(jnp.where(eye, row, 0.0), axis=1, keepdims=True)

    def routes():
        upper = (
            lax.broadcasted_iota(jnp.int32, (tok, tok), 0) < lax.broadcasted_iota(jnp.int32, (tok, tok), 1)
        ).astype(BF16)
        chosen, weight = [], []
        for b in range(ne):
            tile = meta[b // 2, b % 2]
            hit = tile[0:topk, 0:tok] == e.astype(F32)
            chosen.append(jnp.sum(jnp.where(hit, 1.0, 0.0), axis=0, keepdims=True))
            weight.append(jnp.sum(jnp.where(hit, tile[topk : 2 * topk, 0:tok], 0.0), axis=0, keepdims=True))
        choose = jnp.concatenate(chosen, axis=0)
        position = jnp.dot(choose.astype(BF16), upper, preferred_element_type=F32)
        slots = jnp.where(choose > 0.0, position, -1.0)
        return [slots[b : b + 1, :] for b in range(ne)], weight

    def pick(slot_rows, gate_rows):
        for b in range(ne):
            rows_b = lax.dot_general(
                placer(slot_rows[b]), hidden[b * cap : (b + 1) * cap, :], (((0,), (0,)), ((), ())),
                preferred_element_type=F32,
            )
            ht[b // 2, b % 2] = rows_b.astype(BF16)
            gh[b // 2, b % 2] = (to_col(gate_rows[b]) * rows_b).astype(BF16)
        ght[...] = gh[...].reshape(T, F).astype(F32).T.astype(BF16)

    def begin_grads(j):
        gathered(1 + j)
        right = cot_all[j].reshape(T, cw)

        def block_of(b):
            return jnp.dot(ght[w_rows(b), :], right, preferred_element_type=F32)

        if j < summed:
            for k in range(2):
                wg_send1[j, k] = block_of(((r + k) % 2) * 2 + 1 - c).astype(BF16)
            g1[j] = remote(wg_send1.at[j], wg_recv1.at[j], g1_s.at[j], g1_r.at[j], pair_c)
            wg_hold[j] = block_of((1 - r) * 2 + c)
            wg_own[j] = block_of(r * 2 + c)
            return
        s = j - summed
        gathered(1 + C + s)
        if s == 0:
            hy[0].wait_recv()
        far = cot_far[s].reshape(T, cw)

        def both(core):
            other = jnp.dot(ght_far[w_rows(core), :], far, preferred_element_type=F32)
            return block_of(r * 2 + core) + other

        wg_send1[j, 0] = both(1 - c).astype(BF16)
        g1[j] = remote(wg_send1.at[j, 0], wg_recv1.at[j, 0], g1_s.at[j], g1_r.at[j], pair_c)
        wg_own[j] = both(c)

    def pass_grads(j):
        g1[j].wait_recv()
        wg_send2[j] = (wg_hold[j] + wg_recv1[j, 1].astype(F32)).astype(BF16)
        g2[j] = remote(wg_send2.at[j], wg_recv2.at[j], g2_s.at[j], g2_r.at[j], pair_y)

    def out_part(j):
        for d in range(2):
            wf[d, j].wait_recv()
        left = gh[:, pl.ds(1 - x, 1)].reshape(N * tok, F)
        val = jnp.dot(left, wfull[j], preferred_element_type=F32)
        mx_send1[j] = val.astype(BF16).reshape(N, tok, cw)
        m1[j] = remote(mx_send1.at[j], mx_recv1.at[j], m1_s.at[j], m1_r.at[j], pair_e)
        left = gh[:, pl.ds(x, 1)].reshape(N * tok, F)
        val = jnp.dot(left, wfull[j], preferred_element_type=F32)
        mx_own[j] = val.reshape(N, tok, cw)

    def z_part(j):
        gathered(1 + j)
        val = lax.dot_general(
            cot_all[j].reshape(T, cw), wfull[j], (((1,), (1,)), ((), ())), preferred_element_type=F32
        )
        z[...] = val if j == 0 else z[...] + val

    def mix_part(j):
        m1[j].wait_recv()
        for k in order:
            o = (q + k) % N
            mx_send2[j, o] = (mx_own[j, o] + mx_recv1[j, o].astype(F32)).astype(BF16)
            m2[k, j] = remote(
                mx_send2.at[j, o], mx_recv2.at[j, q], m2_s.at[k - 1, j], m2_r.at[k - 1, j],
                to(a, o * 2 + x),
            )

    def hidden_part(slot_rows, gate_rows):
        for b in range(ne):
            zb = z[b * tok : (b + 1) * tok, :]
            gg_col = jnp.sum(ht[b // 2, b % 2].astype(F32) * zb, axis=1, keepdims=True)
            gg_send[b // 2, b % 2, 0:1, 0:tok] = to_row(gg_col)
            scaled = (to_col(gate_rows[b]) * zb).astype(BF16)
            hidden_grads[b * cap : (b + 1) * cap, :] = jnp.dot(
                placer(slot_rows[b]), scaled, preferred_element_type=F32
            ).astype(BF16)
        for d in range(1, ne):
            o = (e + d) % ne
            gg[d] = remote(
                gg_send.at[o // 2, o % 2], gg_recv.at[q, x], gg_s.at[d - 1], gg_r.at[d - 1], to(a, o)
            )
        gg_recv[q, x] = gg_send[q, x]

    far_items = [1 + C + s for s in range(S)]
    half = C // 2
    for i in range(C + 1):
        step(i, 1)
    for i in range(half + 1):
        step(i, 2)
    forward_w(0)
    for i in range(half + 1, C + 1):
        step(i, 2)
    for i in range(half + 1):
        for d in range(3, N):
            step(i, d)
    own_h.wait()
    gathered(0)
    slot_rows, gate_rows = routes()
    pick(slot_rows, gate_rows)
    if S:
        there_rows = pl.ds(pl.multiple_of((1 - r) * 2 * rows, 2 * rows), 2 * rows)
        hy[0] = remote(ght.at[there_rows], ght_far, hy_s.at[0], hy_r.at[0], pair_y)
    out_part(0)
    forward_w(1)
    for i in range(half + 1, C + 1):
        for d in range(3, N):
            step(i, d)
    begin_grads(0)
    out_part(1)
    for s in range(S):
        cy[s].wait_recv()
        begin(far_items[s])
    z_part(0)
    pass_grads(0)
    begin_grads(1)
    z_part(1)
    for i in far_items:
        step(i, 1)
    mix_part(0)
    pass_grads(1)
    for d in range(2, N):
        for i in far_items:
            step(i, d)
    forward_w(2)
    out_part(2)
    mix_part(1)
    if summed > 2:
        begin_grads(2)
    z_part(2)
    if summed > 2:
        pass_grads(2)
    forward_w(3)
    out_part(3)
    mix_part(2)
    if summed > 3:
        begin_grads(3)
    z_part(3)
    if summed > 3:
        pass_grads(3)
    hidden_part(slot_rows, gate_rows)
    mix_part(3)
    for j in range(summed, C):
        begin_grads(j)

    for j in range(C):
        total = mx_own[j, q] + mx_recv1[j, q].astype(F32)
        for k in order:
            m2[k, j].wait_recv()
            total = total + mx_recv2[j, (q - k + N) % N].astype(F32)
        mixed[:, cols(j)] = total.astype(BF16)

    for d in range(1, ne):
        gg[d].wait_recv()
    for k in range(topk):
        row = jnp.zeros((1, tok), F32)
        for b in range(ne):
            row = row + jnp.where(idf[k : k + 1, :] == float(b), gg_recv[b // 2, b % 2, 0:1, 0:tok], 0.0)
        gate_grads[k : k + 1, :] = row

    for j in range(summed, C):
        g1[j].wait_recv()
        weight_grads[:, cols(j)] = (wg_own[j] + wg_recv1[j, 0].astype(F32)).astype(BF16)
    for j in range(summed):
        val = wg_own[j] + wg_recv1[j, 0].astype(F32)
        g2[j].wait_recv()
        weight_grads[:, cols(j)] = (val + wg_recv2[j].astype(F32)).astype(BF16)

    for group in (wy, wf, cy, g1, g2, m1, m2, gg, hy):
        for copy in group.values():
            copy.wait_send()
    for i in range(1 + C + S):
        sent(i)


def store_kernel(count, *refs):
    sems = refs[-1]
    copies = [pltpu.make_async_copy(refs[i], refs[count + i], sems.at[i]) for i in range(count)]
    for copy in copies:
        copy.start()
    for copy in copies:
        copy.wait()


def fused(hidden, weight_rows, expert_ids, gates, cotangent):
    nd, ne = lax.axis_size("dp"), lax.axis_size("expert")
    rows, D = weight_rows.shape
    tok, topk = expert_ids.shape
    F = hidden.shape[1]
    T, N = ne * tok, ne // 2
    C, S = 4, 2
    cw, items, summed = D // C, 1 + C + S, C - S
    vm = pltpu.VMEM
    sem = lambda *n: pltpu.SemaphoreType.DMA(tuple(max(i, 1) for i in n))
    near, far = pl.BlockSpec(memory_space=pltpu.VMEM), pl.BlockSpec(memory_space=pltpu.HBM)
    shapes = [((tok, D), BF16), ((topk, tok), F32), (hidden.shape, BF16), ((rows, D), BF16)]
    few, some = max(S, 1), max(summed, 1)
    tall = -(-2 * topk // 8) * 8
    result_bytes = 2 * (tok * D + hidden.size + rows * D) + 128 * 1024
    results = pl.pallas_call(
        functools.partial(kernel, nd, ne, C, S),
        out_shape=tuple(pltpu.VMEM(*s) for s in shapes),
        in_specs=[far, far, near, near, far],
        out_specs=(near,) * 4,
        scratch_shapes=[
            vm(hidden.shape, BF16), vm((C, F, cw), BF16), vm((C, N, 2, tok, cw), BF16),
            vm((few, N, 2, tok, cw), BF16), vm((N, 2, tall, 128), F32),
            vm((N, 2, 8, 128), F32), vm((N, 2, 8, 128), F32),
            vm((N, 2, tok, F), BF16), vm((N, 2, tok, F), BF16), vm((F, T), BF16), vm((2 * rows, T), BF16),
            vm((T, F), F32),
            vm((C, 2, rows, cw), BF16), vm((C, 2, rows, cw), BF16),
            vm((some, rows, cw), BF16), vm((some, rows, cw), BF16), vm((C, rows, cw), F32),
            vm((some, rows, cw), F32),
            vm((C, N, tok, cw), BF16), vm((C, N, tok, cw), BF16),
            vm((C, N, tok, cw), BF16), vm((C, N, tok, cw), BF16), vm((C, N, tok, cw), F32),
            sem(C), sem(C), sem(2, C), sem(2, C),
            sem(items, 2, N - 1), sem(items, 2, N - 1), sem(items, N), sem(items, N),
            sem(S), sem(S), sem(1), sem(1), sem(ne - 1), sem(ne - 1),
            sem(C), sem(C), sem(summed), sem(summed),
            sem(C), sem(C), sem(N - 1, C), sem(N - 1, C), sem(C), sem(C), sem(1),
        ],
        compiler_params=pltpu.CompilerParams(
            collective_id=0, has_side_effects=True, vmem_limit_bytes=VMEM_BYTES - result_bytes
        ),
    )(hidden, weight_rows, expert_ids.T, gates.T, cotangent)
    mixed, gate_grads, hidden_grads, sums = pl.pallas_call(
        functools.partial(store_kernel, len(shapes)),
        out_shape=tuple(jax.ShapeDtypeStruct(*s) for s in shapes),
        in_specs=[pl.BlockSpec(memory_space=pl.ANY)] * 4,
        out_specs=(far,) * 4,
        scratch_shapes=[sem(len(shapes))],
        compiler_params=pltpu.CompilerParams(vmem_limit_bytes=1024 * 1024),
    )(*results)
    return mixed, gate_grads.T, hidden_grads, sums


def slot_table(expert_ids, experts, capacity):
    flat_ids = expert_ids.reshape(-1)
    choose = (flat_ids[:, None] == jnp.arange(experts, dtype=jnp.int32)[None, :]).astype(jnp.int32)
    earlier = jnp.cumsum(choose, axis=0) - choose
    position = jnp.sum(earlier * choose, axis=1)
    target = flat_ids * capacity + position
    return (target[None, :] == jnp.arange(experts * capacity, dtype=jnp.int32)[:, None]).astype(BF16)


def plain(hidden, weight_rows, expert_ids, gates, cotangent):
    experts = lax.axis_size("expert")
    capacity = hidden.shape[0] // experts
    tok, topk = expert_ids.shape
    width = cotangent.shape[1]
    table = slot_table(expert_ids, experts, capacity)
    weight = lax.all_gather(weight_rows, "dp", axis=0, tiled=True)
    outputs = jnp.dot(hidden, weight, preferred_element_type=F32).astype(BF16)
    back = lax.all_to_all(outputs, "expert", split_axis=0, concat_axis=0, tiled=True)
    picked = lax.dot_general(table, back, (((0,), (0,)), ((), ())), preferred_element_type=F32)
    picked = picked.reshape(tok, topk, width)
    cot32 = cotangent.astype(F32)[:, None, :]
    mixed = jnp.sum(gates[:, :, None] * picked, axis=1).astype(BF16)
    gate_grads = jnp.sum(picked * cot32, axis=2)
    routed = (gates[:, :, None] * cot32).astype(BF16).reshape(-1, width)
    packed = jnp.dot(table, routed, preferred_element_type=F32).astype(BF16)
    grads = lax.all_to_all(packed, "expert", split_axis=0, concat_axis=0, tiled=True)
    hidden_grads = lax.dot_general(
        grads, weight, (((1,), (1,)), ((), ())), preferred_element_type=F32
    ).astype(BF16)
    partial = lax.dot_general(
        hidden, grads, (((0,), (0,)), ((), ())), preferred_element_type=F32
    ).astype(BF16)
    sums = lax.psum_scatter(partial, "dp", scatter_dimension=0, tiled=True)
    return mixed, gate_grads, hidden_grads, sums


def per_device(hidden, w_down, expert_ids, gates, cotangent):
    nd, ne = lax.axis_size("dp"), lax.axis_size("expert")
    rows, width = w_down.shape[1:]
    cap, tok = hidden.shape[0] // ne, expert_ids.shape[0]
    tiled = rows % 16 == 0 and cap % 16 == 0 and tok % 16 == 0 and tok <= 128
    paired = nd == 4 and ne % 2 == 0 and width % 512 == 0
    small = expert_ids.shape[1] <= 8
    body = fused if tiled and paired and small else plain
    mixed, gate_grads, hidden_grads, sums = body(
        hidden, w_down.reshape(rows, width), expert_ids, gates, cotangent
    )
    return mixed, gate_grads, hidden_grads, sums.reshape(1, rows, width)


def solution(mesh):
    split = P(("dp", "expert"), None)
    weights = P("expert", "dp", None)
    return jax.shard_map(
        per_device,
        mesh=mesh,
        in_specs=(split, weights, split, split, split),
        out_specs=(split, split, split, weights),
        check_vma=False,
    )
```

time: 46.2 us -> 47 us (1.017)
  Pallas kernels: 45.4 us -> 46.1 us
    pallas_call x1, Pallas kernels: 44.3 us -> 45.1 us  [fused(): pl.pallas_call(functools.partial(kernel, nd, ne, C, S), out_shape=tuple((...]
where the time goes in v1:
time: 47 us; the launch traced here: 46.8 us
  Pallas kernels  46.1 us (98%)
  between operations  0.64 us (1%)
    pallas_call x1, Pallas kernels, fused(): pl.pallas_call(functools.partial(kernel, nd, ne, C, S), out_shape=tuple((...  45.1 us
    pallas_call x1, Pallas kernels, fused(): pl.pallas_call(functools.partial(store_kernel, len(shapes)), out_shape=tu...  1.09 us

profile of v1, /device:TPU:0, one launch (start us, length us, event | category | flops | bytes accessed | tf_op | source)
XLA Modules:
  0.0 46.8 jit_solution(13247230459574726747)
XLA Ops:
  0.6 45.1 %shard_map.84 = (bf16[32,2048]{1,0:T(8,128)(2,1)S(1)}, f32[4,32]{1,0:T(4,128)S(1)}, bf16[256,768]{1,0:T(8,128)(2,1)S(1)}, bf16[192,2048]{1,0:T(8,128)(2,1)S(1)}) custom-call(bf16[256,768]{1,0:T(8,128)(2,1)} %hidden_in.1, bf16[192,2048]{1,0:T(8,128)(2,1)} %bitcast.5, s32[4,32]{1,0:T(4,128)} %bitcast.6, f32[4,32]{1,0:T(4,128)} %bitcast.7, bf16[32,2048]{1,0:T(8,128)(2,1)} %cot.1), custom_call_target="tpu_custom_call" | custom-call | tf_op jit(solution)/shard_map/pallas_call | solution.py:414
  45.7 1.1 %shard_map.85 = (bf16[32,2048]{1,0:T(8,128)(2,1)}, f32[4,32]{1,0:T(4,128)}, bf16[256,768]{1,0:T(8,128)(2,1)}, bf16[192,2048]{1,0:T(8,128)(2,1)}) custom-call(bf16[32,2048]{1,0:T(8,128)(2,1)S(1)} %get-tuple-element.12.refs_0_, f32[4,32]{1,0:T(4,128)S(1)} %get-tuple-element.13.refs_1_, bf16[256,768]{1,0:T(8,128)(2,1)S(1)} %get-tuple-element.14.refs_2_, ...), custom_call_target="tpu_custom_call" | custom-call | tf_op jit(solution)/shard_map/pallas_call | solution.py:440

commit v2 on v1

v2 whole, which is shorter than its diff:
```python
import functools

import jax
import jax.numpy as jnp
from jax import lax
from jax.experimental import pallas as pl
from jax.experimental.pallas import tpu as pltpu
from jax.sharding import PartitionSpec as P

MESH = pl.DeviceIdType.MESH
F32 = jnp.float32
BF16 = jnp.bfloat16


VMEM_BYTES = 67043328


def kernel(
    nd, ne, C, S, K,
    hidden_in, w, ids, gates, cot,
    mixed, gate_grads, hidden_grads, weight_grads,
    hidden, wfull, cot_all, cot_far, meta, gg_send, gg_recv,
    ht, gh, ght, ght_far, z, wg_send1, wg_recv1, wg_part, wg_recvp, wg_send2, wg_recv2, wg_own, wg_hold,
    mx_send1, mx_recv1, mx_send2, mx_recv2, mx_own,
    wy_s, wy_r, wf_s, wf_r, zs, zr, xs, xr, zms, zmr, xms, xmr, zfs, zfr, xfs, xfr, cy_s, cy_r, hy_s, hy_r, gg_s, gg_r,
    g1_s, g1_r, g2_s, g2_r, m1_s, m1_r, m2_s, m2_r, local,
):
    N = ne // 2
    rows, D = w.shape
    topk, tok = ids.shape
    F = hidden.shape[1]
    cap = hidden.shape[0] // ne
    T, cw, vw = ne * tok, D // C, D // K
    summed = C - S
    a, e = lax.axis_index("dp"), lax.axis_index("expert")
    r, c = a // 2, a % 2
    q, x = e // 2, e % 2

    def to(a2, e2):
        return {"dp": a2, "expert": e2}

    pair_e, pair_c, pair_y = to(a, q * 2 + 1 - x), to(r * 2 + 1 - c, e), to((1 - r) * 2 + c, e)
    ahead, behind = to(a, ((q + 1) % N) * 2 + x), to(a, ((q + N - 1) % N) * 2 + x)
    not_last, not_first = q + 1 < N, q > 0
    onward = ((not_last, ahead), (not_first, behind))

    def copy_of(src, dst, ss, rs, dev):
        return pltpu.make_async_remote_copy(
            src_ref=src, dst_ref=dst, send_sem=ss, recv_sem=rs, device_id=dev, device_id_type=MESH
        )

    def start(src, dst, ss, rs, dev):
        copy_of(src, dst, ss, rs, dev).start()

    def arrived(ref, sem):
        copy_of(ref, ref, sem, sem, pair_e).wait_recv()

    def left(ref, sem):
        copy_of(ref, ref, sem, sem, pair_e).wait_send()

    def w_rows(block):
        return pl.ds(pl.multiple_of(block * rows, rows), rows)

    def cols(j, width=cw):
        return slice(j * width, (j + 1) * width)

    barrier = pltpu.get_barrier_semaphore()
    for dev in (pair_y, pair_c, pair_e):
        pl.semaphore_signal(barrier, inc=1, device_id=dev, device_id_type=MESH)
    for exists, dev in onward:

        @pl.when(exists)
        def _():
            pl.semaphore_signal(barrier, inc=1, device_id=dev, device_id_type=MESH)

    for j in range(K):
        pltpu.make_async_copy(w.at[:, cols(j, vw)], wfull.at[j, w_rows(a)], local.at[0]).start()
    for j in range(C):
        pltpu.make_async_copy(cot.at[:, cols(j)], cot_all.at[j, q, x], local.at[1]).start()
    own_h = pltpu.make_async_copy(hidden_in, hidden, local.at[2])
    own_h.start()

    meta[q, x] = jnp.zeros(meta.shape[2:], F32)
    idf = ids[...].astype(F32)
    meta[q, x, 0:topk, 0:tok] = idf
    meta[q, x, topk : 2 * topk, 0:tok] = gates[...]
    gg_send[...] = jnp.zeros_like(gg_send)

    mine, theirs = w_rows(a), w_rows((1 - r) * 2 + c)
    pltpu.make_async_copy(wfull.at[:, mine], wfull.at[:, mine], local.at[0]).wait()
    own_c = cot_all.at[:, q, x]
    pltpu.make_async_copy(own_c, own_c, local.at[1]).wait()
    pl.semaphore_wait(barrier, 3 + not_last.astype(jnp.int32) + not_first.astype(jnp.int32))

    def there(side, d):
        return q + d < N if side else q >= d

    def at(side, d):
        return q + d if side else q - d

    def pair_of(p, zq):
        return meta.at[zq] if p < 0 else cot_far.at[p, zq]

    def pass_pair(p, side, d):
        zq = at(side, d)
        ref = pair_of(p, zq)
        if p < 0:
            start(ref, ref, zms.at[side, d], zmr.at[zq], onward[side][1])
        else:
            start(ref, ref, zfs.at[side, d], zfr.at[p, zq], onward[side][1])

    def pass_cot(i, side, d):
        ref = cot_all.at[i, at(side, d), x]
        start(ref, ref, zs.at[side, d], zr.at[i, at(side, d)], onward[side][1])

    def across(i, zq):
        ref = cot_all.at[i, zq, x]
        start(ref, ref, xs.at[0], xr.at[i], pair_e)

    def pair_cross(p):
        ref = pair_of(p, q).at[x]
        if p < 0:
            start(ref, ref, xms.at[0], xmr.at[0], pair_e)
        else:
            start(ref, ref, xfs.at[0], xfr.at[p], pair_e)

    def pair_step(p, d):
        if d == 0:
            arrived(pair_of(p, q).at[1 - x], xmr.at[0] if p < 0 else xfr.at[p])
        for side in range(2):

            @pl.when(there(side, d) if d else onward[side][0])
            def _():
                if d:
                    arrived(pair_of(p, at(side, d)), zmr.at[at(side, d)] if p < 0 else zfr.at[p, at(side, d)])
                if 0 < d < N - 1:

                    @pl.when(onward[side][0])
                    def _():
                        pass_pair(p, side, d)

                if d == 0:
                    pass_pair(p, side, d)

    def begin(i):
        for side in range(2):

            @pl.when(onward[side][0])
            def _():
                pass_cot(i, side, 0)

    def step(i, d):
        for side in range(2):

            @pl.when(there(side, d))
            def _():
                arrived(cot_all.at[i, at(side, d), x], zr.at[i, at(side, d)])
                if d < N - 1:

                    @pl.when(onward[side][0])
                    def _():
                        pass_cot(i, side, d)

                across(i, at(side, d))

    def begin_far():
        arrived(cot_far.at[:, q, x], cy_r.at[0])
        for s in range(S):
            pair_cross(s)

    complete = set()

    def gathered(i):
        if i not in complete:
            complete.add(i)
            arrived(cot_all.at[i, :, 1 - x], xr.at[i])

    order = sorted(range(1, N), key=lambda d: min(d, N - d))

    def send_w(j):
        ref = wfull.at[j, mine]
        start(ref, ref, wy_s.at[0], wy_r.at[j], pair_y)

    def share_w(j):
        ref = wfull.at[j, mine]
        start(ref, ref, wf_s.at[0], wf_r.at[j], pair_c)

    def forward_w(j):
        ref = wfull.at[j, theirs]
        arrived(ref, wy_r.at[j])
        start(ref, ref, wf_s.at[0], wf_r.at[j], pair_c)

    def send_far():
        start(
            cot_all.at[summed:C, q, x], cot_far.at[:, q, x], cy_s.at[0], cy_r.at[0], pair_y
        )

    def placer(slot_row):
        return (lax.broadcasted_iota(jnp.int32, (cap, tok), 0).astype(F32) == slot_row).astype(BF16)

    eye = lax.broadcasted_iota(jnp.int32, (tok, tok), 0) == lax.broadcasted_iota(jnp.int32, (tok, tok), 1)

    def to_row(col):
        return jnp.sum(jnp.where(eye, col, 0.0), axis=0, keepdims=True)

    def to_col(row):
        return jnp.sum(jnp.where(eye, row, 0.0), axis=1, keepdims=True)

    def routes():
        upper = (
            lax.broadcasted_iota(jnp.int32, (tok, tok), 0) < lax.broadcasted_iota(jnp.int32, (tok, tok), 1)
        ).astype(BF16)
        chosen, weight = [], []
        for b in range(ne):
            tile = meta[b // 2, b % 2]
            hit = tile[0:topk, 0:tok] == e.astype(F32)
            chosen.append(jnp.sum(jnp.where(hit, 1.0, 0.0), axis=0, keepdims=True))
            weight.append(jnp.sum(jnp.where(hit, tile[topk : 2 * topk, 0:tok], 0.0), axis=0, keepdims=True))
        choose = jnp.concatenate(chosen, axis=0)
        position = jnp.dot(choose.astype(BF16), upper, preferred_element_type=F32)
        slots = jnp.where(choose > 0.0, position, -1.0)
        return [slots[b : b + 1, :] for b in range(ne)], weight

    def pick(slot_rows, gate_rows):
        for b in range(ne):
            rows_b = lax.dot_general(
                placer(slot_rows[b]), hidden[b * cap : (b + 1) * cap, :], (((0,), (0,)), ((), ())),
                preferred_element_type=F32,
            )
            ht[b // 2, b % 2] = rows_b.astype(BF16)
            gh[b // 2, b % 2] = (to_col(gate_rows[b]) * rows_b).astype(BF16)
        ght[...] = gh[...].reshape(T, F).astype(F32).T.astype(BF16)

    def send_rows():
        there_rows = pl.ds(pl.multiple_of((1 - r) * 2 * rows, 2 * rows), 2 * rows)
        start(ght.at[there_rows], ght_far, hy_s.at[0], hy_r.at[0], pair_y)

    def block_of(j, b):
        return jnp.dot(ght[w_rows(b), :], cot_all[j].reshape(T, cw), preferred_element_type=F32)

    def begin_grads(j):
        gathered(j)
        for k in range(2):
            wg_send1[j, k] = block_of(j, ((r + k) % 2) * 2 + 1 - c).astype(BF16)
        start(wg_send1.at[j], wg_recv1.at[j], g1_s.at[0], g1_r.at[j], pair_c)
        wg_hold[j] = block_of(j, (1 - r) * 2 + c)
        wg_own[j] = block_of(j, r * 2 + c)

    def pass_grads(j):
        arrived(wg_recv1.at[j], g1_r.at[j])
        wg_send2[j] = (wg_hold[j] + wg_recv1[j, 1].astype(F32)).astype(BF16)
        start(wg_send2.at[j], wg_recv2.at[j], g2_s.at[0], g2_r.at[j], pair_y)

    def full_grads(j):
        s = j - summed
        gathered(j)
        if s == 0:
            arrived(ght_far, hy_r.at[0])

        def both(core):
            other = jnp.dot(
                ght_far[w_rows(core), :], cot_far[s].reshape(T, cw), preferred_element_type=F32
            )
            return block_of(j, r * 2 + core) + other

        wg_part[s] = both(1 - c).astype(BF16)
        start(wg_part.at[s], wg_recvp.at[s], g1_s.at[1], g1_r.at[j], pair_c)
        wg_own[j] = both(c)

    def out_part(j):
        arrived(wfull.at[j, 0 : 2 * rows], wf_r.at[j])
        lhs = gh[:, pl.ds(1 - x, 1)].reshape(N * tok, F)
        val = jnp.dot(lhs, wfull[j], preferred_element_type=F32)
        mx_send1[j] = val.astype(BF16).reshape(N, tok, vw)
        start(mx_send1.at[j], mx_recv1.at[j], m1_s.at[0], m1_r.at[j], pair_e)
        lhs = gh[:, pl.ds(x, 1)].reshape(N * tok, F)
        val = jnp.dot(lhs, wfull[j], preferred_element_type=F32)
        mx_own[j] = val.reshape(N, tok, vw)

    def z_part(j):
        i = j * vw // cw
        gathered(i)
        part = cot_all[i, :, :, :, cols(j % (cw // vw), vw)].reshape(T, vw)
        val = lax.dot_general(part, wfull[j], (((1,), (1,)), ((), ())), preferred_element_type=F32)
        z[...] = val if j == 0 else z[...] + val

    def mix_part(j):
        arrived(mx_recv1.at[j], m1_r.at[j])
        for k in order:
            o = (q + k) % N
            mx_send2[j, o] = (mx_own[j, o] + mx_recv1[j, o].astype(F32)).astype(BF16)
            start(mx_send2.at[j, o], mx_recv2.at[j, q], m2_s.at[0], m2_r.at[j], to(a, o * 2 + x))

    def hidden_part(slot_rows, gate_rows):
        for b in range(ne):
            zb = z[b * tok : (b + 1) * tok, :]
            gg_col = jnp.sum(ht[b // 2, b % 2].astype(F32) * zb, axis=1, keepdims=True)
            gg_send[b, 0:1, 0:tok] = to_row(gg_col)
            scaled = (to_col(gate_rows[b]) * zb).astype(BF16)
            hidden_grads[b * cap : (b + 1) * cap, :] = jnp.dot(
                placer(slot_rows[b]), scaled, preferred_element_type=F32
            ).astype(BF16)
        for d in range(1, ne):
            o = (e + d) % ne
            start(gg_send.at[o], gg_recv.at[e], gg_s.at[0], gg_r.at[0], to(a, o))
        gg_recv[e] = gg_send[e]

    def finish_mixed(j):
        arrived(mx_recv2.at[j, 0 : N - 1], m2_r.at[j])
        total = mx_own[j, q] + mx_recv1[j, q].astype(F32)
        for k in order:
            total = total + mx_recv2[j, (q - k + N) % N].astype(F32)
        mixed[:, cols(j, vw)] = total.astype(BF16)

    def finish_gates():
        arrived(gg_recv.at[0 : ne - 1], gg_r.at[0])
        for k in range(topk):
            row = jnp.zeros((1, tok), F32)
            for b in range(ne):
                row = row + jnp.where(idf[k : k + 1, :] == float(b), gg_recv[b, 0:1, 0:tok], 0.0)
            gate_grads[k : k + 1, :] = row

    def finish_grads(j):
        if j >= summed:
            arrived(wg_recvp.at[j - summed], g1_r.at[j])
            weight_grads[:, cols(j)] = (wg_own[j] + wg_recvp[j - summed].astype(F32)).astype(BF16)
            return
        val = wg_own[j] + wg_recv1[j, 0].astype(F32)
        arrived(wg_recv2.at[j], g2_r.at[j])
        weight_grads[:, cols(j)] = (val + wg_recv2[j].astype(F32)).astype(BF16)

    pair_cross(-1)
    send_far()
    for j in range(K):
        send_w(j)
    for j in range(C):
        across(j, q)
    begin(0)
    begin(1)
    for j in range(K):
        share_w(j)
    pair_step(-1, 0)
    begin(2)
    begin(3)
    begin_far()
    step(0, 1)
    step(1, 1)
    pair_step(-1, 1)
    step(2, 1)
    step(3, 1)
    step(0, 2)
    step(1, 2)
    pair_step(-1, 2)
    forward_w(0)
    pair_step(0, 0)
    step(2, 2)
    step(3, 2)
    pair_step(1, 0)
    step(0, 3)
    step(1, 3)
    pair_step(-1, 3)
    own_h.wait()
    slot_rows, gate_rows = routes()
    pick(slot_rows, gate_rows)
    forward_w(1)
    out_part(0)
    send_rows()
    forward_w(2)
    step(2, 3)
    step(3, 3)
    forward_w(3)
    out_part(1)
    forward_w(4)
    out_part(2)
    out_part(3)
    mix_part(0)
    forward_w(5)
    pair_step(0, 1)
    out_part(4)
    pair_step(1, 1)
    z_part(0)
    z_part(1)
    forward_w(6)
    mix_part(1)
    out_part(5)
    begin_grads(0)
    forward_w(7)
    mix_part(2)
    pair_step(0, 2)
    out_part(6)
    mix_part(3)
    pair_step(1, 2)
    pass_grads(0)
    out_part(7)
    mix_part(4)
    z_part(2)
    z_part(3)
    z_part(4)
    mix_part(5)
    z_part(5)
    z_part(6)
    z_part(7)
    mix_part(6)
    hidden_part(slot_rows, gate_rows)
    begin_grads(1)
    mix_part(7)
    pass_grads(1)
    pair_step(0, 3)
    full_grads(2)
    pair_step(1, 3)
    full_grads(3)
    for j in range(K - 2):
        finish_mixed(j)
    finish_gates()
    finish_grads(2)
    finish_mixed(K - 2)
    finish_mixed(K - 1)
    finish_grads(0)
    finish_grads(3)
    finish_grads(1)

    left(wfull.at[:, mine], wy_s.at[0])
    left(wfull.at[:, 0 : 2 * rows], wf_s.at[0])
    left(cot_far.at[:, 0, 0], cy_s.at[0])
    left(cot_all.at[:, :, 0], xs.at[0])
    left(cot_far.at[:, 0, 0], xfs.at[0])
    left(meta.at[0, 0], xms.at[0])
    left(ght_far, hy_s.at[0])
    for side in range(2):
        for d in range(N - 1):

            @pl.when(onward[side][0] & there(side, d))
            def _():
                left(meta.at[0], zms.at[side, d])
                left(cot_all.at[:, 0, 0], zs.at[side, d])
                left(cot_far.at[:, 0], zfs.at[side, d])

    left(wg_send1, g1_s.at[0])
    left(wg_part, g1_s.at[1])
    left(mx_send1, m1_s.at[0])
    left(gg_send.at[0 : ne - 1], gg_s.at[0])
    left(mx_send2.at[:, 0 : N - 1], m2_s.at[0])
    left(wg_send2, g2_s.at[0])


def store_kernel(count, *refs):
    sems = refs[-1]
    copies = [pltpu.make_async_copy(refs[i], refs[count + i], sems.at[i]) for i in range(count)]
    for copy in copies:
        copy.start()
    for copy in copies:
        copy.wait()


def fused(hidden, weight_rows, expert_ids, gates, cotangent):
    nd, ne = lax.axis_size("dp"), lax.axis_size("expert")
    rows, D = weight_rows.shape
    tok, topk = expert_ids.shape
    F = hidden.shape[1]
    T, N = ne * tok, ne // 2
    C, S, K = 4, 2, 8
    cw, vw, summed = D // C, D // K, C - S
    vm = pltpu.VMEM
    sem = lambda *n: pltpu.SemaphoreType.DMA(tuple(max(i, 1) for i in n))
    near, far = pl.BlockSpec(memory_space=pltpu.VMEM), pl.BlockSpec(memory_space=pltpu.HBM)
    shapes = [((tok, D), BF16), ((topk, tok), F32), (hidden.shape, BF16), ((rows, D), BF16)]
    tall = -(-2 * topk // 8) * 8
    result_bytes = 2 * (tok * D + hidden.size + rows * D) + 128 * 1024
    results = pl.pallas_call(
        functools.partial(kernel, nd, ne, C, S, K),
        out_shape=tuple(pltpu.VMEM(*s) for s in shapes),
        in_specs=[far, far, near, near, far],
        out_specs=(near,) * 4,
        scratch_shapes=[
            vm(hidden.shape, BF16), vm((K, F, vw), BF16), vm((C, N, 2, tok, cw), BF16),
            vm((S, N, 2, tok, cw), BF16),
            vm((N, 2, tall, 128), F32), vm((ne, 8, 128), F32), vm((ne, 8, 128), F32),
            vm((N, 2, tok, F), BF16), vm((N, 2, tok, F), BF16), vm((F, T), BF16), vm((2 * rows, T), BF16),
            vm((T, F), F32),
            vm((summed, 2, rows, cw), BF16), vm((summed, 2, rows, cw), BF16),
            vm((S, rows, cw), BF16), vm((S, rows, cw), BF16),
            vm((summed, rows, cw), BF16), vm((summed, rows, cw), BF16), vm((C, rows, cw), F32),
            vm((summed, rows, cw), F32),
            vm((K, N, tok, vw), BF16), vm((K, N, tok, vw), BF16),
            vm((K, N, tok, vw), BF16), vm((K, N, tok, vw), BF16), vm((K, N, tok, vw), F32),
            sem(1), sem(K), sem(1), sem(K),
            sem(2, N - 1), sem(C, N), sem(1), sem(C),
            sem(2, N - 1), sem(N), sem(1), sem(1), sem(2, N - 1), sem(S, N), sem(1), sem(S),
            sem(1), sem(1), sem(1), sem(1), sem(1), sem(1),
            sem(2), sem(C), sem(1), sem(summed),
            sem(1), sem(K), sem(1), sem(K), sem(3),
        ],
        compiler_params=pltpu.CompilerParams(
            collective_id=0, has_side_effects=True, vmem_limit_bytes=VMEM_BYTES - result_bytes
        ),
    )(hidden, weight_rows, expert_ids.T, gates.T, cotangent)
    mixed, gate_grads, hidden_grads, sums = pl.pallas_call(
        functools.partial(store_kernel, len(shapes)),
        out_shape=tuple(jax.ShapeDtypeStruct(*s) for s in shapes),
        in_specs=[pl.BlockSpec(memory_space=pl.ANY)] * 4,
        out_specs=(far,) * 4,
        scratch_shapes=[sem(len(shapes))],
        compiler_params=pltpu.CompilerParams(vmem_limit_bytes=1024 * 1024),
    )(*results)
    return mixed, gate_grads.T, hidden_grads, sums


def slot_table(expert_ids, experts, capacity):
    flat_ids = expert_ids.reshape(-1)
    choose = (flat_ids[:, None] == jnp.arange(experts, dtype=jnp.int32)[None, :]).astype(jnp.int32)
    earlier = jnp.cumsum(choose, axis=0) - choose
    position = jnp.sum(earlier * choose, axis=1)
    target = flat_ids * capacity + position
    return (target[None, :] == jnp.arange(experts * capacity, dtype=jnp.int32)[:, None]).astype(BF16)


def plain(hidden, weight_rows, expert_ids, gates, cotangent):
    experts = lax.axis_size("expert")
    capacity = hidden.shape[0] // experts
    tok, topk = expert_ids.shape
    width = cotangent.shape[1]
    table = slot_table(expert_ids, experts, capacity)
    weight = lax.all_gather(weight_rows, "dp", axis=0, tiled=True)
    outputs = jnp.dot(hidden, weight, preferred_element_type=F32).astype(BF16)
    back = lax.all_to_all(outputs, "expert", split_axis=0, concat_axis=0, tiled=True)
    picked = lax.dot_general(table, back, (((0,), (0,)), ((), ())), preferred_element_type=F32)
    picked = picked.reshape(tok, topk, width)
    cot32 = cotangent.astype(F32)[:, None, :]
    mixed = jnp.sum(gates[:, :, None] * picked, axis=1).astype(BF16)
    gate_grads = jnp.sum(picked * cot32, axis=2)
    routed = (gates[:, :, None] * cot32).astype(BF16).reshape(-1, width)
    packed = jnp.dot(table, routed, preferred_element_type=F32).astype(BF16)
    grads = lax.all_to_all(packed, "expert", split_axis=0, concat_axis=0, tiled=True)
    hidden_grads = lax.dot_general(
        grads, weight, (((1,), (1,)), ((), ())), preferred_element_type=F32
    ).astype(BF16)
    partial = lax.dot_general(
        hidden, grads, (((0,), (0,)), ((), ())), preferred_element_type=F32
    ).astype(BF16)
    sums = lax.psum_scatter(partial, "dp", scatter_dimension=0, tiled=True)
    return mixed, gate_grads, hidden_grads, sums


def per_device(hidden, w_down, expert_ids, gates, cotangent):
    nd, ne = lax.axis_size("dp"), lax.axis_size("expert")
    rows, width = w_down.shape[1:]
    cap, tok = hidden.shape[0] // ne, expert_ids.shape[0]
    tiled = rows % 16 == 0 and cap % 16 == 0 and tok % 16 == 0 and tok <= 128
    paired = nd == 4 and ne % 2 == 0 and width % 512 == 0
    small = expert_ids.shape[1] <= 8
    body = fused if tiled and paired and small else plain
    mixed, gate_grads, hidden_grads, sums = body(
        hidden, w_down.reshape(rows, width), expert_ids, gates, cotangent
    )
    return mixed, gate_grads, hidden_grads, sums.reshape(1, rows, width)


def solution(mesh):
    split = P(("dp", "expert"), None)
    weights = P("expert", "dp", None)
    return jax.shard_map(
        per_device,
        mesh=mesh,
        in_specs=(split, weights, split, split, split),
        out_specs=(split, split, split, weights),
        check_vma=False,
    )
```

time: 47 us -> 41.1 us (0.87)
  Pallas kernels: 46.1 us -> 40.2 us
    pallas_call x1, Pallas kernels: 45.1 us -> 39.2 us  [fused(): pl.pallas_call(functools.partial(kernel, nd, ne, C, S, K), out_shape=tupl...]
where the time goes in v2:
time: 41.1 us; the launch traced here: 40.9 us
  Pallas kernels  40.2 us (98%)
  between operations  0.64 us (2%)
    pallas_call x1, Pallas kernels, fused(): pl.pallas_call(functools.partial(kernel, nd, ne, C, S, K), out_shape=tupl...  39.2 us
    pallas_call x1, Pallas kernels, fused(): pl.pallas_call(functools.partial(store_kernel, len(shapes)), out_shape=tu...  1.09 us

profile of v2, /device:TPU:0, one launch (start us, length us, event | category | flops | bytes accessed | tf_op | source)
XLA Modules:
  0.0 40.9 jit_solution(12886322045352065727)
XLA Ops:
  0.6 39.2 %shard_map.84 = (bf16[32,2048]{1,0:T(8,128)(2,1)S(1)}, f32[4,32]{1,0:T(4,128)S(1)}, bf16[256,768]{1,0:T(8,128)(2,1)S(1)}, bf16[192,2048]{1,0:T(8,128)(2,1)S(1)}) custom-call(bf16[256,768]{1,0:T(8,128)(2,1)} %hidden_in.1, bf16[192,2048]{1,0:T(8,128)(2,1)} %bitcast.5, s32[4,32]{1,0:T(4,128)} %bitcast.6, f32[4,32]{1,0:T(4,128)} %bitcast.7, bf16[32,2048]{1,0:T(8,128)(2,1)} %cot.1), custom_call_target="tpu_custom_call" | custom-call | tf_op jit(solution)/shard_map/pallas_call | solution.py:469
  39.8 1.1 %shard_map.85 = (bf16[32,2048]{1,0:T(8,128)(2,1)}, f32[4,32]{1,0:T(4,128)}, bf16[256,768]{1,0:T(8,128)(2,1)}, bf16[192,2048]{1,0:T(8,128)(2,1)}) custom-call(bf16[32,2048]{1,0:T(8,128)(2,1)S(1)} %get-tuple-element.12.refs_0_, f32[4,32]{1,0:T(4,128)S(1)} %get-tuple-element.13.refs_1_, bf16[256,768]{1,0:T(8,128)(2,1)S(1)} %get-tuple-element.14.refs_2_, ...), custom_call_target="tpu_custom_call" | custom-call | tf_op jit(solution)/shard_map/pallas_call | solution.py:497

commit v3 on v2

--- a/solution.py
+++ b/solution.py
@@ -16,14 +16,14 @@
 
 
 def kernel(
-    nd, ne, C, S, K,
-    hidden_in, w, ids, gates, cot,
+    nd, ne, C, S, K, groups,
+    hidden_in, w, ids_in, gates_in, cot,
     mixed, gate_grads, hidden_grads, weight_grads,
-    hidden, wfull, cot_all, cot_far, meta, gg_send, gg_recv,
+    ids, gates, hidden, wfull, cot_all, cot_far, meta, gg_send, gg_recv,
     ht, gh, ght, ght_far, z, wg_send1, wg_recv1, wg_part, wg_recvp, wg_send2, wg_recv2, wg_own, wg_hold,
     mx_send1, mx_recv1, mx_send2, mx_recv2, mx_own,
-    wy_s, wy_r, wf_s, wf_r, zs, zr, xs, xr, zms, zmr, xms, xmr, zfs, zfr, xfs, xfr, cy_s, cy_r, hy_s, hy_r, gg_s, gg_r,
-    g1_s, g1_r, g2_s, g2_r, m1_s, m1_r, m2_s, m2_r, local,
+    wy_r, wf_r, zr, xr, zmr, xmr, cy_r, hy_r, gg_r,
+    g1_r, g2_r, m1_r, m2_r, out_w, out_x, out_g, out_t, out_gg, ready,
 ):
     N = ne // 2
     rows, D = w.shape
@@ -73,23 +73,29 @@
         def _():
             pl.semaphore_signal(barrier, inc=1, device_id=dev, device_id_type=MESH)
 
+    own_ids = pltpu.make_async_copy(ids_in, ids, out_t.at[0])
+    own_gates = pltpu.make_async_copy(gates_in, gates, out_g.at[0])
+    own_ids.start()
+    own_gates.start()
     for j in range(K):
-        pltpu.make_async_copy(w.at[:, cols(j, vw)], wfull.at[j, w_rows(a)], local.at[0]).start()
+        pltpu.make_async_copy(w.at[:, cols(j, vw)], wfull.at[j, w_rows(a)], out_w.at[0]).start()
     for j in range(C):
-        pltpu.make_async_copy(cot.at[:, cols(j)], cot_all.at[j, q, x], local.at[1]).start()
-    own_h = pltpu.make_async_copy(hidden_in, hidden, local.at[2])
+        pltpu.make_async_copy(cot.at[:, cols(j)], cot_all.at[j, q, x], out_x.at[0]).start()
+    own_h = pltpu.make_async_copy(hidden_in, hidden, out_gg.at[0])
     own_h.start()
 
     meta[q, x] = jnp.zeros(meta.shape[2:], F32)
+    gg_send[...] = jnp.zeros_like(gg_send)
+    own_ids.wait()
+    own_gates.wait()
     idf = ids[...].astype(F32)
     meta[q, x, 0:topk, 0:tok] = idf
     meta[q, x, topk : 2 * topk, 0:tok] = gates[...]
-    gg_send[...] = jnp.zeros_like(gg_send)
 
     mine, theirs = w_rows(a), w_rows((1 - r) * 2 + c)
-    pltpu.make_async_copy(wfull.at[:, mine], wfull.at[:, mine], local.at[0]).wait()
+    pltpu.make_async_copy(wfull.at[:, mine], wfull.at[:, mine], out_w.at[0]).wait()
     own_c = cot_all.at[:, q, x]
-    pltpu.make_async_copy(own_c, own_c, local.at[1]).wait()
+    pltpu.make_async_copy(own_c, own_c, out_x.at[0]).wait()
     pl.semaphore_wait(barrier, 3 + not_last.astype(jnp.int32) + not_first.astype(jnp.int32))
 
     def there(side, d):
@@ -98,41 +104,60 @@
     def at(side, d):
         return q + d if side else q - d
 
-    def pair_of(p, zq):
-        return meta.at[zq] if p < 0 else cot_far.at[p, zq]
+    def place(side, d):
+        return q + d - 1 if side else d - 1
+
+    def place_next(side, d):
+        return q - 1 + d if side else d
 
     def pass_pair(p, side, d):
-        zq = at(side, d)
-        ref = pair_of(p, zq)
-        if p < 0:
-            start(ref, ref, zms.at[side, d], zmr.at[zq], onward[side][1])
-        else:
-            start(ref, ref, zfs.at[side, d], zfr.at[p, zq], onward[side][1])
+        ref = cot_far.at[p, at(side, d)]
+        start(ref, ref, out_x.at[0], zr.at[C + p, place_next(side, d)], onward[side][1])
 
     def pass_cot(i, side, d):
         ref = cot_all.at[i, at(side, d), x]
-        start(ref, ref, zs.at[side, d], zr.at[i, at(side, d)], onward[side][1])
+        start(ref, ref, out_x.at[0], zr.at[i, place_next(side, d)], onward[side][1])
 
     def across(i, zq):
         ref = cot_all.at[i, zq, x]
-        start(ref, ref, xs.at[0], xr.at[i], pair_e)
-
-    def pair_cross(p):
-        ref = pair_of(p, q).at[x]
-        if p < 0:
-            start(ref, ref, xms.at[0], xmr.at[0], pair_e)
-        else:
-            start(ref, ref, xfs.at[0], xfr.at[p], pair_e)
+        start(ref, ref, out_x.at[0], xr.at[i], pair_e)
+
+    def tell(d):
+        for side in range(2):
+
+            @pl.when(there(side, d - 1) & onward[side][0])
+            def _():
+                pl.semaphore_signal(
+                    ready.at[side, d - 2], inc=1, device_id=onward[side][1], device_id_type=MESH
+                )
+
+    def hear(d):
+        for side in range(2):
+
+            @pl.when(there(side, d))
+            def _():
+                pl.semaphore_wait(ready.at[side, d - 2], 1)
+
+    def tiles_cross():
+        start(meta.at[q, x], meta.at[q, x], out_t.at[0], xmr.at[0], pair_e)
+
+    def tiles_out():
+        arrived(meta.at[q, 1 - x], xmr.at[0])
+        for d in order:
+            start(meta.at[q], meta.at[q], out_t.at[0], zmr.at[0], to(a, ((q + d) % N) * 2 + x))
+
+    def tiles_in():
+        arrived(meta.at[0 : N - 1], zmr.at[0])
 
     def pair_step(p, d):
         if d == 0:
-            arrived(pair_of(p, q).at[1 - x], xmr.at[0] if p < 0 else xfr.at[p])
+            arrived(cot_far.at[p, q, 1 - x], xr.at[C + p])
         for side in range(2):
 
             @pl.when(there(side, d) if d else onward[side][0])
             def _():
                 if d:
-                    arrived(pair_of(p, at(side, d)), zmr.at[at(side, d)] if p < 0 else zfr.at[p, at(side, d)])
+                    arrived(cot_far.at[p, at(side, d)], zr.at[C + p, place(side, d)])
                 if 0 < d < N - 1:
 
                     @pl.when(onward[side][0])
@@ -154,7 +179,7 @@
 
             @pl.when(there(side, d))
             def _():
-                arrived(cot_all.at[i, at(side, d), x], zr.at[i, at(side, d)])
+                arrived(cot_all.at[i, at(side, d), x], zr.at[i, place(side, d)])
                 if d < N - 1:
 
                     @pl.when(onward[side][0])
@@ -166,7 +191,8 @@
     def begin_far():
         arrived(cot_far.at[:, q, x], cy_r.at[0])
         for s in range(S):
-            pair_cross(s)
+            ref = cot_far.at[s, q, x]
+            start(ref, ref, out_x.at[0], xr.at[C + s], pair_e)
 
     complete = set()
 
@@ -177,22 +203,22 @@
 
     order = sorted(range(1, N), key=lambda d: min(d, N - d))
 
-    def send_w(j):
-        ref = wfull.at[j, mine]
-        start(ref, ref, wy_s.at[0], wy_r.at[j], pair_y)
-
-    def share_w(j):
-        ref = wfull.at[j, mine]
-        start(ref, ref, wf_s.at[0], wf_r.at[j], pair_c)
-
-    def forward_w(j):
-        ref = wfull.at[j, theirs]
-        arrived(ref, wy_r.at[j])
-        start(ref, ref, wf_s.at[0], wf_r.at[j], pair_c)
+    def send_w(k):
+        ref = wfull.at[slice(*groups[k]), mine]
+        start(ref, ref, out_w.at[0], wy_r.at[k], pair_y)
+
+    def share_w(k):
+        ref = wfull.at[slice(*groups[k]), mine]
+        start(ref, ref, out_w.at[0], wf_r.at[k], pair_c)
+
+    def forward_w(k):
+        ref = wfull.at[slice(*groups[k]), theirs]
+        arrived(ref, wy_r.at[k])
+        start(ref, ref, out_w.at[0], wf_r.at[k], pair_c)
 
     def send_far():
         start(
-            cot_all.at[summed:C, q, x], cot_far.at[:, q, x], cy_s.at[0], cy_r.at[0], pair_y
+            cot_all.at[summed:C, q, x], cot_far.at[:, q, x], out_x.at[0], cy_r.at[0], pair_y
         )
 
     def placer(slot_row):
@@ -233,7 +259,7 @@
 
     def send_rows():
         there_rows = pl.ds(pl.multiple_of((1 - r) * 2 * rows, 2 * rows), 2 * rows)
-        start(ght.at[there_rows], ght_far, hy_s.at[0], hy_r.at[0], pair_y)
+        start(ght.at[there_rows], ght_far, out_g.at[0], hy_r.at[0], pair_y)
 
     def block_of(j, b):
         return jnp.dot(ght[w_rows(b), :], cot_all[j].reshape(T, cw), preferred_element_type=F32)
@@ -242,14 +268,14 @@
         gathered(j)
         for k in range(2):
             wg_send1[j, k] = block_of(j, ((r + k) % 2) * 2 + 1 - c).astype(BF16)
-        start(wg_send1.at[j], wg_recv1.at[j], g1_s.at[0], g1_r.at[j], pair_c)
+        start(wg_send1.at[j], wg_recv1.at[j], out_g.at[0], g1_r.at[j], pair_c)
         wg_hold[j] = block_of(j, (1 - r) * 2 + c)
         wg_own[j] = block_of(j, r * 2 + c)
 
     def pass_grads(j):
         arrived(wg_recv1.at[j], g1_r.at[j])
         wg_send2[j] = (wg_hold[j] + wg_recv1[j, 1].astype(F32)).astype(BF16)
-        start(wg_send2.at[j], wg_recv2.at[j], g2_s.at[0], g2_r.at[j], pair_y)
+        start(wg_send2.at[j], wg_recv2.at[j], out_g.at[0], g2_r.at[j], pair_y)
 
     def full_grads(j):
         s = j - summed
@@ -264,32 +290,41 @@
             return block_of(j, r * 2 + core) + other
 
         wg_part[s] = both(1 - c).astype(BF16)
-        start(wg_part.at[s], wg_recvp.at[s], g1_s.at[1], g1_r.at[j], pair_c)
+        start(wg_part.at[s], wg_recvp.at[s], out_g.at[0], g1_r.at[j], pair_c)
         wg_own[j] = both(c)
 
-    def out_part(j):
-        arrived(wfull.at[j, 0 : 2 * rows], wf_r.at[j])
+    def out_part(k):
+        piece = slice(*groups[k])
+        arrived(wfull.at[piece, 0 : 2 * rows], wf_r.at[k])
         lhs = gh[:, pl.ds(1 - x, 1)].reshape(N * tok, F)
-        val = jnp.dot(lhs, wfull[j], preferred_element_type=F32)
-        mx_send1[j] = val.astype(BF16).reshape(N, tok, vw)
-        start(mx_send1.at[j], mx_recv1.at[j], m1_s.at[0], m1_r.at[j], pair_e)
+        for j in range(*groups[k]):
+            val = jnp.dot(lhs, wfull[j], preferred_element_type=F32)
+            mx_send1[j] = val.astype(BF16).reshape(N, tok, vw)
+        start(mx_send1.at[piece], mx_recv1.at[piece], out_x.at[0], m1_r.at[k], pair_e)
         lhs = gh[:, pl.ds(x, 1)].reshape(N * tok, F)
-        val = jnp.dot(lhs, wfull[j], preferred_element_type=F32)
-        mx_own[j] = val.reshape(N, tok, vw)
-
-    def z_part(j):
-        i = j * vw // cw
-        gathered(i)
-        part = cot_all[i, :, :, :, cols(j % (cw // vw), vw)].reshape(T, vw)
-        val = lax.dot_general(part, wfull[j], (((1,), (1,)), ((), ())), preferred_element_type=F32)
-        z[...] = val if j == 0 else z[...] + val
-
-    def mix_part(j):
-        arrived(mx_recv1.at[j], m1_r.at[j])
-        for k in order:
-            o = (q + k) % N
-            mx_send2[j, o] = (mx_own[j, o] + mx_recv1[j, o].astype(F32)).astype(BF16)
-            start(mx_send2.at[j, o], mx_recv2.at[j, q], m2_s.at[0], m2_r.at[j], to(a, o * 2 + x))
+        for j in range(*groups[k]):
+            val = jnp.dot(lhs, wfull[j], preferred_element_type=F32)
+            mx_own[j] = val.reshape(N, tok, vw)
+
+    def z_part(k):
+        for j in range(*groups[k]):
+            i = j * vw // cw
+            gathered(i)
+            part = cot_all[i, :, :, :, cols(j % (cw // vw), vw)].reshape(T, vw)
+            val = lax.dot_general(part, wfull[j], (((1,), (1,)), ((), ())), preferred_element_type=F32)
+            z[...] = val if j == 0 else z[...] + val
+
+    early = groups[-2][0]
+
+    def mix_part(k):
+        piece = slice(*groups[k])
+        arrived(mx_recv1.at[piece], m1_r.at[k])
+        sem = m2_r.at[max(0, k - len(groups) + 3)]
+        for d in order:
+            o = (q + d) % N
+            for j in range(*groups[k]):
+                mx_send2[j, o] = (mx_own[j, o] + mx_recv1[j, o].astype(F32)).astype(BF16)
+            start(mx_send2.at[piece, o], mx_recv2.at[piece, q], out_x.at[0], sem, to(a, o * 2 + x))
 
     def hidden_part(slot_rows, gate_rows):
         for b in range(ne):
@@ -302,15 +337,17 @@
             ).astype(BF16)
         for d in range(1, ne):
             o = (e + d) % ne
-            start(gg_send.at[o], gg_recv.at[e], gg_s.at[0], gg_r.at[0], to(a, o))
+            start(gg_send.at[o], gg_recv.at[e], out_gg.at[0], gg_r.at[0], to(a, o))
         gg_recv[e] = gg_send[e]
 
-    def finish_mixed(j):
-        arrived(mx_recv2.at[j, 0 : N - 1], m2_r.at[j])
-        total = mx_own[j, q] + mx_recv1[j, q].astype(F32)
-        for k in order:
-            total = total + mx_recv2[j, (q - k + N) % N].astype(F32)
-        mixed[:, cols(j, vw)] = total.astype(BF16)
+    def finish_mixed(k):
+        first, last = (0, early) if k == 0 else groups[k - 3]
+        arrived(mx_recv2.at[first:last, 0 : N - 1], m2_r.at[k])
+        for j in range(first, last):
+            total = mx_own[j, q] + mx_recv1[j, q].astype(F32)
+            for d in order:
+                total = total + mx_recv2[j, (q - d + N) % N].astype(F32)
+            mixed[:, cols(j, vw)] = total.astype(BF16)
 
     def finish_gates():
         arrived(gg_recv.at[0 : ne - 1], gg_r.at[0])
@@ -329,118 +366,99 @@
         arrived(wg_recv2.at[j], g2_r.at[j])
         weight_grads[:, cols(j)] = (val + wg_recv2[j].astype(F32)).astype(BF16)
 
-    pair_cross(-1)
+    tiles_cross()
     send_far()
-    for j in range(K):
-        send_w(j)
+    for k in range(len(groups)):
+        send_w(k)
     for j in range(C):
         across(j, q)
     begin(0)
     begin(1)
-    for j in range(K):
-        share_w(j)
-    pair_step(-1, 0)
+    for d in range(2, N):
+        tell(d)
+        if d == 2:
+            for k in range(len(groups)):
+                share_w(k)
+        hear(d)
+    tiles_out()
     begin(2)
     begin(3)
     begin_far()
     step(0, 1)
     step(1, 1)
-    pair_step(-1, 1)
     step(2, 1)
     step(3, 1)
+    pair_step(0, 0)
+    forward_w(0)
     step(0, 2)
     step(1, 2)
-    pair_step(-1, 2)
-    forward_w(0)
-    pair_step(0, 0)
+    own_h.wait()
+    tiles_in()
+    slot_rows, gate_rows = routes()
+    pick(slot_rows, gate_rows)
+    send_rows()
+    out_part(0)
     step(2, 2)
     step(3, 2)
     pair_step(1, 0)
     step(0, 3)
+    forward_w(1)
     step(1, 3)
-    pair_step(-1, 3)
-    own_h.wait()
-    slot_rows, gate_rows = routes()
-    pick(slot_rows, gate_rows)
-    forward_w(1)
-    out_part(0)
-    send_rows()
-    forward_w(2)
+    out_part(1)
     step(2, 3)
     step(3, 3)
+    pair_step(0, 1)
+    forward_w(2)
+    mix_part(0)
+    pair_step(1, 1)
     forward_w(3)
-    out_part(1)
+    out_part(2)
+    begin_grads(0)
     forward_w(4)
-    out_part(2)
     out_part(3)
-    mix_part(0)
+    mix_part(1)
     forward_w(5)
-    pair_step(0, 1)
+    begin_grads(1)
+    pass_grads(0)
     out_part(4)
-    pair_step(1, 1)
+    pair_step(0, 2)
+    mix_part(2)
+    out_part(5)
+    pair_step(1, 2)
+    mix_part(3)
     z_part(0)
     z_part(1)
-    forward_w(6)
-    mix_part(1)
-    out_part(5)
-    begin_grads(0)
-    forward_w(7)
-    mix_part(2)
-    pair_step(0, 2)
-    out_part(6)
-    mix_part(3)
-    pair_step(1, 2)
-    pass_grads(0)
-    out_part(7)
-    mix_part(4)
     z_part(2)
     z_part(3)
     z_part(4)
-    mix_part(5)
     z_part(5)
-    z_part(6)
-    z_part(7)
-    mix_part(6)
     hidden_part(slot_rows, gate_rows)
-    begin_grads(1)
-    mix_part(7)
+    mix_part(4)
     pass_grads(1)
     pair_step(0, 3)
+    mix_part(5)
     full_grads(2)
     pair_step(1, 3)
     full_grads(3)
-    for j in range(K - 2):
-        finish_mixed(j)
+    finish_mixed(0)
     finish_gates()
     finish_grads(2)
-    finish_mixed(K - 2)
-    finish_mixed(K - 1)
     finish_grads(0)
+    finish_mixed(1)
+    finish_grads(1)
     finish_grads(3)
-    finish_grads(1)
-
-    left(wfull.at[:, mine], wy_s.at[0])
-    left(wfull.at[:, 0 : 2 * rows], wf_s.at[0])
-    left(cot_far.at[:, 0, 0], cy_s.at[0])
-    left(cot_all.at[:, :, 0], xs.at[0])
-    left(cot_far.at[:, 0, 0], xfs.at[0])
-    left(meta.at[0, 0], xms.at[0])
-    left(ght_far, hy_s.at[0])
-    for side in range(2):
-        for d in range(N - 1):
-
-            @pl.when(onward[side][0] & there(side, d))
-            def _():
-                left(meta.at[0], zms.at[side, d])
-                left(cot_all.at[:, 0, 0], zs.at[side, d])
-                left(cot_far.at[:, 0], zfs.at[side, d])
-
-    left(wg_send1, g1_s.at[0])
-    left(wg_part, g1_s.at[1])
-    left(mx_send1, m1_s.at[0])
-    left(gg_send.at[0 : ne - 1], gg_s.at[0])
-    left(mx_send2.at[:, 0 : N - 1], m2_s.at[0])
-    left(wg_send2, g2_s.at[0])
+    finish_mixed(2)
+
+    left(wfull.at[:, 0 : 3 * rows], out_w.at[0])
+    left(wfull.at[:, 0 : 2 * rows + 2 * rows * T // D], out_g.at[0])
+    for inner in range(2):
+
+        @pl.when((not_first & not_last) if inner else ~(not_first & not_last))
+        def _():
+            left(wfull.at[:, 0 : 3 * N * tok + 2 * tok * (N + 1 if inner else 1)], out_x.at[0])
+
+    left(gg_recv.at[0 : 2 * N - 1], out_t.at[0])
+    left(gg_send.at[0 : ne - 1], out_gg.at[0])
 
 
 def store_kernel(count, *refs):
@@ -459,6 +477,8 @@
     F = hidden.shape[1]
     T, N = ne * tok, ne // 2
     C, S, K = 4, 2, 8
+    groups = ((0, 2), (2, 4), (4, 5), (5, 6), (6, 7), (7, 8))
+    G = len(groups)
     cw, vw, summed = D // C, D // K, C - S
     vm = pltpu.VMEM
     sem = lambda *n: pltpu.SemaphoreType.DMA(tuple(max(i, 1) for i in n))
@@ -467,12 +487,12 @@
     tall = -(-2 * topk // 8) * 8
     result_bytes = 2 * (tok * D + hidden.size + rows * D) + 128 * 1024
     results = pl.pallas_call(
-        functools.partial(kernel, nd, ne, C, S, K),
+        functools.partial(kernel, nd, ne, C, S, K, groups),
         out_shape=tuple(pltpu.VMEM(*s) for s in shapes),
-        in_specs=[far, far, near, near, far],
+        in_specs=[far] * 5,
         out_specs=(near,) * 4,
         scratch_shapes=[
-            vm(hidden.shape, BF16), vm((K, F, vw), BF16), vm((C, N, 2, tok, cw), BF16),
+            vm((topk, tok), jnp.int32), vm((topk, tok), F32), vm(hidden.shape, BF16), vm((K, F, vw), BF16), vm((C, N, 2, tok, cw), BF16),
             vm((S, N, 2, tok, cw), BF16),
             vm((N, 2, tall, 128), F32), vm((ne, 8, 128), F32), vm((ne, 8, 128), F32),
             vm((N, 2, tok, F), BF16), vm((N, 2, tok, F), BF16), vm((F, T), BF16), vm((2 * rows, T), BF16),
@@ -483,12 +503,9 @@
             vm((summed, rows, cw), F32),
             vm((K, N, tok, vw), BF16), vm((K, N, tok, vw), BF16),
             vm((K, N, tok, vw), BF16), vm((K, N, tok, vw), BF16), vm((K, N, tok, vw), F32),
-            sem(1), sem(K), sem(1), sem(K),
-            sem(2, N - 1), sem(C, N), sem(1), sem(C),
-            sem(2, N - 1), sem(N), sem(1), sem(1), sem(2, N - 1), sem(S, N), sem(1), sem(S),
-            sem(1), sem(1), sem(1), sem(1), sem(1), sem(1),
-            sem(2), sem(C), sem(1), sem(summed),
-            sem(1), sem(K), sem(1), sem(K), sem(3),
+            sem(G), sem(G), sem(C + S, N - 1), sem(C + S), sem(1), sem(1), sem(1), sem(1), sem(1),
+            sem(C), sem(summed), sem(G), sem(3), sem(1), sem(1), sem(1), sem(1), sem(1),
+            pltpu.SemaphoreType.REGULAR((2, max(N - 2, 1))),
         ],
         compiler_params=pltpu.CompilerParams(
             collective_id=0, has_side_effects=True, vmem_limit_bytes=VMEM_BYTES - result_bytes

time: 41.1 us -> 39 us (0.949)
  Pallas kernels: 40.2 us -> 38.2 us
    pallas_call x1, Pallas kernels: 39.2 us -> 37.1 us  [fused(): pl.pallas_call(functools.partial(kernel, nd, ne, C, S, K, groups), out_sh...]
where the time goes in v3:
time: 39 us; the launch traced here: 38.9 us
  Pallas kernels  38.2 us (98%)
  between operations  0.64 us (2%)
    pallas_call x1, Pallas kernels, fused(): pl.pallas_call(functools.partial(kernel, nd, ne, C, S, K, groups), out_sh...  37.1 us
    pallas_call x1, Pallas kernels, fused(): pl.pallas_call(functools.partial(store_kernel, len(shapes)), out_shape=tu...  1.09 us

profile of v3, /device:TPU:0, one launch (start us, length us, event | category | flops | bytes accessed | tf_op | source)
XLA Modules:
  0.0 38.9 jit_solution(9657370002865266532)
XLA Ops:
  0.6 37.1 %shard_map.84 = (bf16[32,2048]{1,0:T(8,128)(2,1)S(1)}, f32[4,32]{1,0:T(4,128)S(1)}, bf16[256,768]{1,0:T(8,128)(2,1)S(1)}, bf16[192,2048]{1,0:T(8,128)(2,1)S(1)}) custom-call(bf16[256,768]{1,0:T(8,128)(2,1)} %hidden_in.1, bf16[192,2048]{1,0:T(8,128)(2,1)} %bitcast.5, s32[4,32]{1,0:T(4,128)} %bitcast.6, f32[4,32]{1,0:T(4,128)} %bitcast.7, bf16[32,2048]{1,0:T(8,128)(2,1)} %cot.1), custom_call_target="tpu_custom_call" | custom-call | tf_op jit(solution)/shard_map/pallas_call | solution.py:489
  37.8 1.1 %shard_map.85 = (bf16[32,2048]{1,0:T(8,128)(2,1)}, f32[4,32]{1,0:T(4,128)}, bf16[256,768]{1,0:T(8,128)(2,1)}, bf16[192,2048]{1,0:T(8,128)(2,1)}) custom-call(bf16[32,2048]{1,0:T(8,128)(2,1)S(1)} %get-tuple-element.12.refs_0_, f32[4,32]{1,0:T(4,128)S(1)} %get-tuple-element.13.refs_1_, bf16[256,768]{1,0:T(8,128)(2,1)S(1)} %get-tuple-element.14.refs_2_, ...), custom_call_target="tpu_custom_call" | custom-call | tf_op jit(solution)/shard_map/pallas_call | solution.py:514

commit v4 on v3

--- a/solution.py
+++ b/solution.py
@@ -374,6 +374,7 @@
         across(j, q)
     begin(0)
     begin(1)
+    begin(2)
     for d in range(2, N):
         tell(d)
         if d == 2:
@@ -381,17 +382,16 @@
                 share_w(k)
         hear(d)
     tiles_out()
-    begin(2)
     begin(3)
-    begin_far()
     step(0, 1)
     step(1, 1)
+    begin_far()
     step(2, 1)
     step(3, 1)
+    step(0, 2)
+    forward_w(0)
+    step(1, 2)
     pair_step(0, 0)
-    forward_w(0)
-    step(0, 2)
-    step(1, 2)
     own_h.wait()
     tiles_in()
     slot_rows, gate_rows = routes()
@@ -400,9 +400,9 @@
     out_part(0)
     step(2, 2)
     step(3, 2)
-    pair_step(1, 0)
     step(0, 3)
     forward_w(1)
+    pair_step(1, 0)
     step(1, 3)
     out_part(1)
     step(2, 3)
@@ -418,25 +418,25 @@
     out_part(3)
     mix_part(1)
     forward_w(5)
+    out_part(4)
+    pair_step(0, 2)
     begin_grads(1)
     pass_grads(0)
-    out_part(4)
-    pair_step(0, 2)
     mix_part(2)
     out_part(5)
     pair_step(1, 2)
     mix_part(3)
+    pass_grads(1)
     z_part(0)
     z_part(1)
     z_part(2)
+    mix_part(4)
     z_part(3)
     z_part(4)
     z_part(5)
     hidden_part(slot_rows, gate_rows)
-    mix_part(4)
-    pass_grads(1)
+    mix_part(5)
     pair_step(0, 3)
-    mix_part(5)
     full_grads(2)
     pair_step(1, 3)
     full_grads(3)

time: 39 us -> 38.7 us (level)
  no operation moved by 1% of the time
where the time goes in v4:
time: 38.7 us; the launch traced here: 38.5 us
  Pallas kernels  37.9 us (98%)
  between operations  0.64 us (2%)
    pallas_call x1, Pallas kernels, fused(): pl.pallas_call(functools.partial(kernel, nd, ne, C, S, K, groups), out_sh...  36.8 us
    pallas_call x1, Pallas kernels, fused(): pl.pallas_call(functools.partial(store_kernel, len(shapes)), out_shape=tu...  1.09 us

profile of v4, /device:TPU:0, one launch (start us, length us, event | category | flops | bytes accessed | tf_op | source)
XLA Modules:
  0.0 38.5 jit_solution(11444290587208942015)
XLA Ops:
  0.6 36.8 %shard_map.84 = (bf16[32,2048]{1,0:T(8,128)(2,1)S(1)}, f32[4,32]{1,0:T(4,128)S(1)}, bf16[256,768]{1,0:T(8,128)(2,1)S(1)}, bf16[192,2048]{1,0:T(8,128)(2,1)S(1)}) custom-call(bf16[256,768]{1,0:T(8,128)(2,1)} %hidden_in.1, bf16[192,2048]{1,0:T(8,128)(2,1)} %bitcast.5, s32[4,32]{1,0:T(4,128)} %bitcast.6, f32[4,32]{1,0:T(4,128)} %bitcast.7, bf16[32,2048]{1,0:T(8,128)(2,1)} %cot.1), custom_call_target="tpu_custom_call" | custom-call | tf_op jit(solution)/shard_map/pallas_call | solution.py:489
  37.4 1.1 %shard_map.85 = (bf16[32,2048]{1,0:T(8,128)(2,1)}, f32[4,32]{1,0:T(4,128)}, bf16[256,768]{1,0:T(8,128)(2,1)}, bf16[192,2048]{1,0:T(8,128)(2,1)}) custom-call(bf16[32,2048]{1,0:T(8,128)(2,1)S(1)} %get-tuple-element.12.refs_0_, f32[4,32]{1,0:T(4,128)S(1)} %get-tuple-element.13.refs_1_, bf16[256,768]{1,0:T(8,128)(2,1)S(1)} %get-tuple-element.14.refs_2_, ...), custom_call_target="tpu_custom_call" | custom-call | tf_op jit(solution)/shard_map/pallas_call | solution.py:514

commit v5 on v4

--- a/solution.py
+++ b/solution.py
@@ -16,14 +16,15 @@
 
 
 def kernel(
-    nd, ne, C, S, K, groups,
+    nd, ne, C, S, A, K, M, groups,
     hidden_in, w, ids_in, gates_in, cot,
     mixed, gate_grads, hidden_grads, weight_grads,
     ids, gates, hidden, wfull, cot_all, cot_far, meta, gg_send, gg_recv,
     ht, gh, ght, ght_far, z, wg_send1, wg_recv1, wg_part, wg_recvp, wg_send2, wg_recv2, wg_own, wg_hold,
     mx_send1, mx_recv1, mx_send2, mx_recv2, mx_own,
+    sum_own, sum_send, sum_up, sum_down, sum_send2, sum_recv2,
     wy_r, wf_r, zr, xr, zmr, xmr, cy_r, hy_r, gg_r,
-    g1_r, g2_r, m1_r, m2_r, out_w, out_x, out_g, out_t, out_gg, ready,
+    g1_r, g2_r, m1_r, m2_r, up_r, down_r, sum_r, out_w, out_x, out_g, out_t, out_gg, ready,
 ):
     N = ne // 2
     rows, D = w.shape
@@ -31,7 +32,8 @@
     F = hidden.shape[1]
     cap = hidden.shape[0] // ne
     T, cw, vw = ne * tok, D // C, D // K
-    summed = C - S
+    summed, G = C - S, len(groups)
+    lined = sum(last <= M for _, last in groups)
     a, e = lax.axis_index("dp"), lax.axis_index("expert")
     r, c = a // 2, a % 2
     q, x = e // 2, e % 2
@@ -86,6 +88,15 @@
 
     meta[q, x] = jnp.zeros(meta.shape[2:], F32)
     gg_send[...] = jnp.zeros_like(gg_send)
+
+    @pl.when(q == 0)
+    def _():
+        sum_up[:, 0] = jnp.zeros_like(sum_up[:, 0])
+
+    @pl.when(q == N - 1)
+    def _():
+        sum_down[:, N - 1] = jnp.zeros_like(sum_down[:, N - 1])
+
     own_ids.wait()
     own_gates.wait()
     idf = ids[...].astype(F32)
@@ -114,12 +125,15 @@
         ref = cot_far.at[p, at(side, d)]
         start(ref, ref, out_x.at[0], zr.at[C + p, place_next(side, d)], onward[side][1])
 
+    def chunk(i):
+        return cot_all.at[i] if i < C else cot_far.at[i - C]
+
     def pass_cot(i, side, d):
-        ref = cot_all.at[i, at(side, d), x]
+        ref = chunk(i).at[at(side, d), x]
         start(ref, ref, out_x.at[0], zr.at[i, place_next(side, d)], onward[side][1])
 
     def across(i, zq):
-        ref = cot_all.at[i, zq, x]
+        ref = chunk(i).at[zq, x]
         start(ref, ref, out_x.at[0], xr.at[i], pair_e)
 
     def tell(d):
@@ -179,27 +193,31 @@
 
             @pl.when(there(side, d))
             def _():
-                arrived(cot_all.at[i, at(side, d), x], zr.at[i, place(side, d)])
+                arrived(chunk(i).at[at(side, d), x], zr.at[i, place(side, d)])
                 if d < N - 1:
 
                     @pl.when(onward[side][0])
                     def _():
                         pass_cot(i, side, d)
 
-                across(i, at(side, d))
+                if i < C:
+                    across(i, at(side, d))
 
     def begin_far():
         arrived(cot_far.at[:, q, x], cy_r.at[0])
-        for s in range(S):
-            ref = cot_far.at[s, q, x]
-            start(ref, ref, out_x.at[0], xr.at[C + s], pair_e)
+        for s in range(A):
+            across(C + s, q)
+
+    def cross_all(i):
+        for zq in range(N):
+            across(i, zq)
 
     complete = set()
 
     def gathered(i):
         if i not in complete:
             complete.add(i)
-            arrived(cot_all.at[i, :, 1 - x], xr.at[i])
+            arrived(chunk(i).at[:, 1 - x], xr.at[i])
 
     order = sorted(range(1, N), key=lambda d: min(d, N - d))
 
@@ -280,6 +298,8 @@
     def full_grads(j):
         s = j - summed
         gathered(j)
+        if s >= A:
+            gathered(C + s)
         if s == 0:
             arrived(ght_far, hy_r.at[0])
 
@@ -296,11 +316,17 @@
     def out_part(k):
         piece = slice(*groups[k])
         arrived(wfull.at[piece, 0 : 2 * rows], wf_r.at[k])
+        if k < lined:
+            for j in range(*groups[k]):
+                val = jnp.dot(gh[...].reshape(T, F), wfull[j], preferred_element_type=F32)
+                sum_own[j] = val.reshape(N, 2, tok, vw)
+                line_step(j, 0)
+            return
         lhs = gh[:, pl.ds(1 - x, 1)].reshape(N * tok, F)
         for j in range(*groups[k]):
             val = jnp.dot(lhs, wfull[j], preferred_element_type=F32)
             mx_send1[j] = val.astype(BF16).reshape(N, tok, vw)
-        start(mx_send1.at[piece], mx_recv1.at[piece], out_x.at[0], m1_r.at[k], pair_e)
+        start(mx_send1.at[piece], mx_recv1.at[piece], out_x.at[0], m1_r.at[k - lined], pair_e)
         lhs = gh[:, pl.ds(x, 1)].reshape(N * tok, F)
         for j in range(*groups[k]):
             val = jnp.dot(lhs, wfull[j], preferred_element_type=F32)
@@ -314,11 +340,47 @@
             val = lax.dot_general(part, wfull[j], (((1,), (1,)), ((), ())), preferred_element_type=F32)
             z[...] = val if j == 0 else z[...] + val
 
+    def line_step(j, d):
+        last = N - 1 - d
+
+        @pl.when(q == d)
+        def _():
+            if d:
+                arrived(sum_up.at[j, d:N], up_r.at[j])
+            for o in range(d + 1, N):
+                total = sum_own[j, o] + sum_up[j, o].astype(F32) if d else sum_own[j, o]
+                sum_send[j, o] = total.astype(BF16)
+            if d < N - 1:
+                piece = pl.ds(d + 1, N - 1 - d)
+                start(sum_send.at[j, piece], sum_up.at[j, piece], out_x.at[0], up_r.at[j], ahead)
+
+        @pl.when(q == last)
+        def _():
+            if d:
+                arrived(sum_down.at[j, 0 : last + 1], down_r.at[j])
+            for o in range(last):
+                total = sum_own[j, o] + sum_down[j, o].astype(F32) if d else sum_own[j, o]
+                sum_send[j, o] = total.astype(BF16)
+            if last:
+                piece = pl.ds(0, last)
+                start(sum_send.at[j, piece], sum_down.at[j, piece], out_x.at[0], down_r.at[j], behind)
+
+    def line_sum(j, xq):
+        return sum_own[j, q, xq] + sum_up[j, q, xq].astype(F32) + sum_down[j, q, xq].astype(F32)
+
+    def line_cross(j):
+        sum_send2[j] = line_sum(j, 1 - x).astype(BF16)
+        start(sum_send2.at[j], sum_recv2.at[j], out_x.at[0], sum_r.at[j], pair_e)
+
+    def finish_line(j):
+        arrived(sum_recv2.at[j], sum_r.at[j])
+        mixed[:, cols(j, vw)] = (line_sum(j, x) + sum_recv2[j].astype(F32)).astype(BF16)
+
     early = groups[-2][0]
 
     def mix_part(k):
         piece = slice(*groups[k])
-        arrived(mx_recv1.at[piece], m1_r.at[k])
+        arrived(mx_recv1.at[piece], m1_r.at[k - lined])
         sem = m2_r.at[max(0, k - len(groups) + 3)]
         for d in order:
             o = (q + d) % N
@@ -341,7 +403,7 @@
         gg_recv[e] = gg_send[e]
 
     def finish_mixed(k):
-        first, last = (0, early) if k == 0 else groups[k - 3]
+        first, last = (M, early) if k == 0 else groups[k - 3]
         arrived(mx_recv2.at[first:last, 0 : N - 1], m2_r.at[k])
         for j in range(first, last):
             total = mx_own[j, q] + mx_recv1[j, q].astype(F32)
@@ -386,6 +448,7 @@
     step(0, 1)
     step(1, 1)
     begin_far()
+    begin(5)
     step(2, 1)
     step(3, 1)
     step(0, 2)
@@ -400,46 +463,55 @@
     out_part(0)
     step(2, 2)
     step(3, 2)
+    step(5, 1)
     step(0, 3)
     forward_w(1)
-    pair_step(1, 0)
     step(1, 3)
     out_part(1)
+    line_step(0, 1)
     step(2, 3)
+    line_step(1, 1)
     step(3, 3)
+    step(5, 2)
     pair_step(0, 1)
     forward_w(2)
-    mix_part(0)
-    pair_step(1, 1)
     forward_w(3)
     out_part(2)
     begin_grads(0)
+    line_step(0, 2)
     forward_w(4)
     out_part(3)
+    line_step(1, 2)
+    pass_grads(0)
     mix_part(1)
+    step(5, 3)
     forward_w(5)
     out_part(4)
+    begin_grads(1)
     pair_step(0, 2)
-    begin_grads(1)
-    pass_grads(0)
     mix_part(2)
+    z_part(0)
     out_part(5)
-    pair_step(1, 2)
-    mix_part(3)
+    cross_all(5)
     pass_grads(1)
-    z_part(0)
     z_part(1)
     z_part(2)
-    mix_part(4)
+    mix_part(3)
     z_part(3)
     z_part(4)
     z_part(5)
     hidden_part(slot_rows, gate_rows)
+    line_step(0, 3)
+    line_cross(0)
+    mix_part(4)
+    line_step(1, 3)
+    line_cross(1)
     mix_part(5)
     pair_step(0, 3)
     full_grads(2)
-    pair_step(1, 3)
     full_grads(3)
+    for j in range(M):
+        finish_line(j)
     finish_mixed(0)
     finish_gates()
     finish_grads(2)
@@ -451,11 +523,13 @@
 
     left(wfull.at[:, 0 : 3 * rows], out_w.at[0])
     left(wfull.at[:, 0 : 2 * rows + 2 * rows * T // D], out_g.at[0])
+    once = (C * N + A + (S - A) * N + S) * tok // C + (2 * N - 1) * tok
+    each = (C + S + A) * tok // C
     for inner in range(2):
 
         @pl.when((not_first & not_last) if inner else ~(not_first & not_last))
         def _():
-            left(wfull.at[:, 0 : 3 * N * tok + 2 * tok * (N + 1 if inner else 1)], out_x.at[0])
+            left(wfull.at[:, 0 : once + each * (N + 1 if inner else 1)], out_x.at[0])
 
     left(gg_recv.at[0 : 2 * N - 1], out_t.at[0])
     left(gg_send.at[0 : ne - 1], out_gg.at[0])
@@ -476,7 +550,7 @@
     tok, topk = expert_ids.shape
     F = hidden.shape[1]
     T, N = ne * tok, ne // 2
-    C, S, K = 4, 2, 8
+    C, S, A, K, M = 4, 2, 1, 8, 2
     groups = ((0, 2), (2, 4), (4, 5), (5, 6), (6, 7), (7, 8))
     G = len(groups)
     cw, vw, summed = D // C, D // K, C - S
@@ -487,7 +561,7 @@
     tall = -(-2 * topk // 8) * 8
     result_bytes = 2 * (tok * D + hidden.size + rows * D) + 128 * 1024
     results = pl.pallas_call(
-        functools.partial(kernel, nd, ne, C, S, K, groups),
+        functools.partial(kernel, nd, ne, C, S, A, K, M, groups),
         out_shape=tuple(pltpu.VMEM(*s) for s in shapes),
         in_specs=[far] * 5,
         out_specs=(near,) * 4,
@@ -503,8 +577,10 @@
             vm((summed, rows, cw), F32),
             vm((K, N, tok, vw), BF16), vm((K, N, tok, vw), BF16),
             vm((K, N, tok, vw), BF16), vm((K, N, tok, vw), BF16), vm((K, N, tok, vw), F32),
+            vm((M, N, 2, tok, vw), F32), vm((M, N, 2, tok, vw), BF16), vm((M, N, 2, tok, vw), BF16),
+            vm((M, N, 2, tok, vw), BF16), vm((M, tok, vw), BF16), vm((M, tok, vw), BF16),
             sem(G), sem(G), sem(C + S, N - 1), sem(C + S), sem(1), sem(1), sem(1), sem(1), sem(1),
-            sem(C), sem(summed), sem(G), sem(3), sem(1), sem(1), sem(1), sem(1), sem(1),
+            sem(C), sem(summed), sem(G - sum(last <= M for _, last in groups)), sem(3), sem(M), sem(M), sem(M), sem(1), sem(1), sem(1), sem(1), sem(1),
             pltpu.SemaphoreType.REGULAR((2, max(N - 2, 1))),
         ],
         compiler_params=pltpu.CompilerParams(

time: 38.7 us -> 38.7 us (level)
  no operation moved by 1% of the time
where the time goes in v5:
time: 38.7 us; the launch traced here: 38.5 us
  Pallas kernels  37.9 us (98%)
  between operations  0.64 us (2%)
    pallas_call x1, Pallas kernels, fused(): pl.pallas_call(functools.partial(kernel, nd, ne, C, S, A, K, M, groups),...  36.8 us
    pallas_call x1, Pallas kernels, fused(): pl.pallas_call(functools.partial(store_kernel, len(shapes)), out_shape=tu...  1.09 us

profile of v5, /device:TPU:0, one launch (start us, length us, event | category | flops | bytes accessed | tf_op | source)
XLA Modules:
  0.0 38.5 jit_solution(5358649762045868733)
XLA Ops:
  0.6 36.8 %shard_map.84 = (bf16[32,2048]{1,0:T(8,128)(2,1)S(1)}, f32[4,32]{1,0:T(4,128)S(1)}, bf16[256,768]{1,0:T(8,128)(2,1)S(1)}, bf16[192,2048]{1,0:T(8,128)(2,1)S(1)}) custom-call(bf16[256,768]{1,0:T(8,128)(2,1)} %hidden_in.1, bf16[192,2048]{1,0:T(8,128)(2,1)} %bitcast.5, s32[4,32]{1,0:T(4,128)} %bitcast.6, f32[4,32]{1,0:T(4,128)} %bitcast.7, bf16[32,2048]{1,0:T(8,128)(2,1)} %cot.1), custom_call_target="tpu_custom_call" | custom-call | tf_op jit(solution)/shard_map/pallas_call | solution.py:563
  37.4 1.1 %shard_map.85 = (bf16[32,2048]{1,0:T(8,128)(2,1)}, f32[4,32]{1,0:T(4,128)}, bf16[256,768]{1,0:T(8,128)(2,1)}, bf16[192,2048]{1,0:T(8,128)(2,1)}) custom-call(bf16[32,2048]{1,0:T(8,128)(2,1)S(1)} %get-tuple-element.12.refs_0_, f32[4,32]{1,0:T(4,128)S(1)} %get-tuple-element.13.refs_1_, bf16[256,768]{1,0:T(8,128)(2,1)S(1)} %get-tuple-element.14.refs_2_, ...), custom_call_target="tpu_custom_call" | custom-call | tf_op jit(solution)/shard_map/pallas_call | solution.py:590

commit v6 on v5

--- a/solution.py
+++ b/solution.py
@@ -451,10 +451,10 @@
     begin(5)
     step(2, 1)
     step(3, 1)
+    pair_step(0, 0)
     step(0, 2)
     forward_w(0)
     step(1, 2)
-    pair_step(0, 0)
     own_h.wait()
     tiles_in()
     slot_rows, gate_rows = routes()
@@ -465,18 +465,18 @@
     step(3, 2)
     step(5, 1)
     step(0, 3)
+    step(1, 3)
     forward_w(1)
-    step(1, 3)
     out_part(1)
     line_step(0, 1)
     step(2, 3)
     line_step(1, 1)
     step(3, 3)
-    step(5, 2)
     pair_step(0, 1)
     forward_w(2)
+    step(5, 2)
+    out_part(2)
     forward_w(3)
-    out_part(2)
     begin_grads(0)
     line_step(0, 2)
     forward_w(4)
@@ -494,9 +494,9 @@
     out_part(5)
     cross_all(5)
     pass_grads(1)
+    mix_part(3)
     z_part(1)
     z_part(2)
-    mix_part(3)
     z_part(3)
     z_part(4)
     z_part(5)

time: 38.7 us -> 38.6 us (level)
  no operation moved by 1% of the time
where the time goes in v6:
time: 38.6 us; the launch traced here: 38.4 us
  Pallas kernels  37.8 us (98%)
  between operations  0.64 us (2%)
    pallas_call x1, Pallas kernels, fused(): pl.pallas_call(functools.partial(kernel, nd, ne, C, S, A, K, M, groups),...  36.7 us
    pallas_call x1, Pallas kernels, fused(): pl.pallas_call(functools.partial(store_kernel, len(shapes)), out_shape=tu...  1.09 us

profile of v6, /device:TPU:0, one launch (start us, length us, event | category | flops | bytes accessed | tf_op | source)
XLA Modules:
  0.0 38.4 jit_solution(2850369144041871570)
XLA Ops:
  0.6 36.7 %shard_map.84 = (bf16[32,2048]{1,0:T(8,128)(2,1)S(1)}, f32[4,32]{1,0:T(4,128)S(1)}, bf16[256,768]{1,0:T(8,128)(2,1)S(1)}, bf16[192,2048]{1,0:T(8,128)(2,1)S(1)}) custom-call(bf16[256,768]{1,0:T(8,128)(2,1)} %hidden_in.1, bf16[192,2048]{1,0:T(8,128)(2,1)} %bitcast.5, s32[4,32]{1,0:T(4,128)} %bitcast.6, f32[4,32]{1,0:T(4,128)} %bitcast.7, bf16[32,2048]{1,0:T(8,128)(2,1)} %cot.1), custom_call_target="tpu_custom_call" | custom-call | tf_op jit(solution)/shard_map/pallas_call | solution.py:563
  37.3 1.1 %shard_map.85 = (bf16[32,2048]{1,0:T(8,128)(2,1)}, f32[4,32]{1,0:T(4,128)}, bf16[256,768]{1,0:T(8,128)(2,1)}, bf16[192,2048]{1,0:T(8,128)(2,1)}) custom-call(bf16[32,2048]{1,0:T(8,128)(2,1)S(1)} %get-tuple-element.12.refs_0_, f32[4,32]{1,0:T(4,128)S(1)} %get-tuple-element.13.refs_1_, bf16[256,768]{1,0:T(8,128)(2,1)S(1)} %get-tuple-element.14.refs_2_, ...), custom_call_target="tpu_custom_call" | custom-call | tf_op jit(solution)/shard_map/pallas_call | solution.py:590

commit v7 on v6

--- a/solution.py
+++ b/solution.py
@@ -517,9 +517,9 @@
     finish_grads(2)
     finish_grads(0)
     finish_mixed(1)
-    finish_grads(1)
     finish_grads(3)
     finish_mixed(2)
+    finish_grads(1)
 
     left(wfull.at[:, 0 : 3 * rows], out_w.at[0])
     left(wfull.at[:, 0 : 2 * rows + 2 * rows * T // D], out_g.at[0])

time: 38.6 us -> 38.6 us (level)
  no operation moved by 1% of the time
where the time goes in v7:
time: 38.6 us; the launch traced here: 38.5 us
  Pallas kernels  37.8 us (98%)
  between operations  0.64 us (2%)
    pallas_call x1, Pallas kernels, fused(): pl.pallas_call(functools.partial(kernel, nd, ne, C, S, A, K, M, groups),...  36.8 us
    pallas_call x1, Pallas kernels, fused(): pl.pallas_call(functools.partial(store_kernel, len(shapes)), out_shape=tu...  1.09 us

profile of v7, /device:TPU:0, one launch (start us, length us, event | category | flops | bytes accessed | tf_op | source)
XLA Modules:
  0.0 38.5 jit_solution(15630892909991352325)
XLA Ops:
  0.6 36.8 %shard_map.84 = (bf16[32,2048]{1,0:T(8,128)(2,1)S(1)}, f32[4,32]{1,0:T(4,128)S(1)}, bf16[256,768]{1,0:T(8,128)(2,1)S(1)}, bf16[192,2048]{1,0:T(8,128)(2,1)S(1)}) custom-call(bf16[256,768]{1,0:T(8,128)(2,1)} %hidden_in.1, bf16[192,2048]{1,0:T(8,128)(2,1)} %bitcast.5, s32[4,32]{1,0:T(4,128)} %bitcast.6, f32[4,32]{1,0:T(4,128)} %bitcast.7, bf16[32,2048]{1,0:T(8,128)(2,1)} %cot.1), custom_call_target="tpu_custom_call" | custom-call | tf_op jit(solution)/shard_map/pallas_call | solution.py:563
  37.4 1.1 %shard_map.85 = (bf16[32,2048]{1,0:T(8,128)(2,1)}, f32[4,32]{1,0:T(4,128)}, bf16[256,768]{1,0:T(8,128)(2,1)}, bf16[192,2048]{1,0:T(8,128)(2,1)}) custom-call(bf16[32,2048]{1,0:T(8,128)(2,1)S(1)} %get-tuple-element.12.refs_0_, f32[4,32]{1,0:T(4,128)S(1)} %get-tuple-element.13.refs_1_, bf16[256,768]{1,0:T(8,128)(2,1)S(1)} %get-tuple-element.14.refs_2_, ...), custom_call_target="tpu_custom_call" | custom-call | tf_op jit(solution)/shard_map/pallas_call | solution.py:590
